TPU v7x, 512 devices: a whole 4x4x16 slice. The times are simulated.
512 devices in a mesh: dom: 128 (over z, x, core), sub: 4 (over y).
Axes of the slice: x: 4, y: 4, z: 16, core: 2. Of those that a mesh axis runs over, the one named last changes fastest.
Arguments:
- source_one: float32 [25, 327680], P(None, ('dom', 'sub')), may hold values from -17 to 17
- source_two: float32 [25, 327680], P(None, ('dom', 'sub')), may hold values from -17 to 17
- face_mass: float32 [327680], P(('dom', 'sub')), may hold values from 0.2 to 1
- penalty: float32 [131072], P(('dom', 'sub')), may hold values from 0.5 to 2
- interior_scale: float32 [500, 131072], P(None, ('dom', 'sub')), may hold values from 0.5 to 2
- coupling: float32 [500, 150], replicated, may hold values from -0.5 to 0.5
- inverse_block: float32 [500, 500], replicated, as said below
- element_faces: int32 [6, 131072], P(None, ('dom', 'sub')), may hold values from 0 to 3071, as said below
- element_type: int32 [131072], P(('dom', 'sub')), may hold values 0 or 1
- send_faces: int32 [4, 65536], P(None, ('dom', 'sub')), may hold values from 0 to 2559
Outputs:
- trace_two: float32 [25, 327680], P(None, ('dom', 'sub'))
- interior: float32 [500, 131072], P(None, ('dom', 'sub'))
Inputs may be any that keep to these rules, and one draw needn't show every extreme that they name: `element_faces`: every entry of rows 0 to 4 or of row 5 lies below 3072; on each device each of the 512 received faces is named exactly once, always in rows 0 to 4; row 5 names only group faces. `inverse_block`: symmetric positive definite.
All inputs are finite; a program needn't handle non-finite values. No bound on the sum of `element_type` on one device may be relied on, other than what follows from the above.
Results may differ from a plain program's by a relative error of at most 0.0003.
Values sent between devices are 32-bit elements; how exact they have to be, the bound alone decides.
No kernel may reach another device: no remote copies, remote signals or barrier semaphores. Data moves between devices by JAX's collectives and lax.ppermute only.
A program may use at most 64 MiB of HBM per device.

v0:
```python
import jax
import jax.numpy as jnp
from jax import lax
from jax.experimental import pallas as pl
from jax.experimental.pallas import tpu as pltpu
from jax.sharding import Mesh
from jax.sharding import PartitionSpec as P

F32 = jnp.float32
BF16 = jnp.bfloat16
LANES = 128
ROWS = 32
DOM = ("zq", "zr", "x", "core")
ALL = ("zq", "zr", "x", "core", "sub")
NEAR = ("x", "core", "sub")
FAR = ("zq", "zr")
VMEM = pl.BlockSpec(memory_space=pltpu.VMEM)
SMEM = pl.BlockSpec(memory_space=pltpu.SMEM)


def kernel_call(body, outs, *args, specs=None, scratch=()):
    return pl.pallas_call(
        body,
        out_shape=outs,
        in_specs=specs or [VMEM] * len(args),
        out_specs=jax.tree.map(lambda _: VMEM, outs),
        scratch_shapes=scratch,
        compiler_params=pltpu.CompilerParams(vmem_limit_bytes=32 << 20),
    )(*args)


def shape(*dims, dtype=F32):
    return jax.ShapeDtypeStruct(dims, dtype)


def split3(x):
    high = x.astype(BF16)
    rest = x - high.astype(F32)
    middle = rest.astype(BF16)
    low = (rest - middle.astype(F32)).astype(BF16)
    return jnp.concatenate([high, middle, low], axis=0)


def join3(y):
    return y[:ROWS] + y[ROWS : 2 * ROWS] + y[2 * ROWS :]


def halves(x):
    high = x.astype(BF16)
    return high, (x - high.astype(F32)).astype(BF16)


def rounded_halves(x):
    high = lax.reduce_precision(x, exponent_bits=8, mantissa_bits=7)
    return high.astype(BF16), (x - high).astype(BF16)


def product(left, right):
    high, low = halves(right)
    return jnp.dot(left[0][...], high, preferred_element_type=F32) + (
        jnp.dot(left[0][...], low, preferred_element_type=F32)
        + jnp.dot(left[1][...], high, preferred_element_type=F32)
    )


def pick_lanes(index, tiles, groups):
    index = jnp.broadcast_to(index, (8, LANES))
    block = lax.shift_right_logical(index, 7)
    lane = jnp.bitwise_and(index, LANES - 1)
    count, load = tiles
    picked = [jnp.zeros((8, LANES), F32) for _ in range(groups)]
    for source in range(count):
        here = block == source
        for group in range(groups):
            moved = jnp.take_along_axis(load(source, group), lane, axis=1)
            picked[group] = jnp.where(here, moved, picked[group])
    return picked


def place_lanes(pieces, spread, first, width):
    offset = spread - lax.broadcasted_iota(jnp.int32, spread.shape, 1)
    hits = [(offset == (first + k)).astype(F32).astype(BF16) for k in range(0, width, LANES)]
    return join3(jnp.dot(pieces, jnp.concatenate(hits, axis=1), preferred_element_type=F32))


def lane_sums(x):
    total = x[:, :LANES]
    for begin in range(LANES, x.shape[1], LANES):
        total = total + x[:, begin : begin + LANES]
    return jnp.sum(total, axis=0, keepdims=True)


def start_kernel(one, two, mass, outgoing):
    nodes, owned = one.shape
    for member in range(outgoing.shape[0]):
        outgoing[member, :nodes, :] = one[...]
        outgoing[member, nodes:ROWS, :] = jnp.zeros((ROWS - nodes, owned), F32)
        outgoing[member, ROWS : ROWS + nodes, :] = two[...]
        outgoing[member, ROWS + nodes : 2 * ROWS - 1, :] = jnp.zeros((ROWS - 1 - nodes, owned), F32)
        outgoing[member, 2 * ROWS - 1 :, :] = mass[...]


def first_kernel(arrived, send_list, v0, other, *outgoing):
    blocks = arrived.shape[2] // LANES
    for member in range(arrived.shape[0]):
        for block in range(blocks):
            to = pl.ds((member * blocks + block) * LANES, LANES)
            v0[:, to] = arrived[member, :ROWS, pl.ds(block * LANES, LANES)]
            other[:, to] = arrived[member, ROWS:, pl.ds(block * LANES, LANES)]

    def load(source, group):
        member, block = divmod(source, blocks)
        return arrived[member, pl.ds(group * 8, 8), pl.ds(block * LANES, LANES)]

    for channel in range(4):
        index = send_list[:, pl.ds(channel * LANES, LANES)]
        picked = pick_lanes(index, (arrived.shape[0] * blocks, load), 2 * ROWS // 8)
        for group, tile in enumerate(picked):
            outgoing[channel][pl.ds(group * 8, 8), :] = tile


def gather_slots(vector, ghosts, faces, mask, weighted):
    count = vector.shape[1] // LANES
    width = mask.shape[1]
    near = vector[...]
    pieces = split3(jnp.concatenate([near] + [g[:ROWS, :] for g in ghosts], axis=1))

    def load(source, group):
        if source < count:
            return vector[pl.ds(group * 8, 8), pl.ds(source * LANES, LANES)]
        return ghosts[source - count][pl.ds(group * 8, 8), :]

    def step(slot, carry):
        other = slot + 3
        index = faces[:, pl.ds(pl.multiple_of(other * width, LANES), width)]
        lines = lax.broadcasted_iota(jnp.int32, (pieces.shape[1], width), 0)
        hits = (lines == index).astype(F32).astype(BF16)
        values = join3(jnp.dot(pieces, hits, preferred_element_type=F32))
        for block in range(width // LANES):
            begin = pl.multiple_of(slot * width + block * LANES, LANES)
            picked = pick_lanes(faces[:, pl.ds(begin, LANES)], (count + 4, load), ROWS // 8)
            for group, tile in enumerate(picked):
                row = pl.multiple_of(slot * ROWS + group * 8, 8)
                weighted[pl.ds(row, 8), pl.ds(block * LANES, LANES)] = tile
        weighted[pl.ds(pl.multiple_of(other * ROWS, ROWS), ROWS), :] = values
        return carry

    lax.fori_loop(0, 3, step, 0)
    weighted[pl.ds(5 * ROWS, ROWS), :] = weighted[pl.ds(5 * ROWS, ROWS), :] * mask[...]


def apply_kernel(*refs):
    vector, *ghosts = refs[:5]
    faces, spread, mask, penalty = refs[5:9]
    coupling, lift, inverse = refs[9:11], refs[11:13], refs[13:15]
    scale = refs[15]
    returned, pieces, weighted = refs[16:20], refs[20], refs[-1]
    gather_slots(vector, ghosts, faces, mask, weighted)
    w = weighted[...]
    s = scale[...]
    coupled = s * product(coupling, w)
    inside = s * product(inverse, coupled)
    if len(refs) == 23:
        refs[21][...] = inside
    contrib = penalty[...] * w + product(lift, inside)
    slots = [contrib[k * ROWS : (k + 1) * ROWS] for k in range(6)]
    slots[5] = slots[5] * mask[...]
    parts = split3(jnp.concatenate(slots, axis=1))
    pieces[...] = parts
    width = 5 * mask.shape[1]
    for pair in range(2):
        onto = place_lanes(
            parts[:, :width], spread[:width], vector.shape[1] + pair * 2 * LANES, 2 * LANES
        )
        returned[2 * pair][...] = onto[:, :LANES]
        returned[2 * pair + 1][...] = onto[:, LANES:]


def place_kernel(pieces, spread, placed):
    for begin in range(0, placed.shape[1], 2 * LANES):
        placed[:, pl.ds(begin, 2 * LANES)] = place_lanes(
            pieces[...], spread[...], begin, 2 * LANES
        )


def pack_kernel(placed, r0, r1, r2, r3, spread, packed):
    blocks = placed.shape[1] // LANES
    parts = split3(jnp.concatenate([r[...] for r in (r0, r1, r2, r3)], axis=1))
    packed[:, pl.ds(24 * blocks, 24), :] = jnp.zeros((4, 24, LANES), F32)
    for begin in range(0, blocks, 2):
        onto = place_lanes(parts, spread[...], begin * LANES, 2 * LANES)
        onto = onto + placed[:, pl.ds(begin * LANES, 2 * LANES)]
        for k in range(2):
            block = begin + k
            half = onto[:, k * LANES : (k + 1) * LANES]
            for member in range(4):
                for group in range(3):
                    packed[member, pl.ds((group * blocks + block) * 8, 8), :] = half[
                        group * 8 : group * 8 + 8
                    ]
                packed[member, pl.ds(24 * blocks + block, 1), :] = half[24:25]


def next_kernel(arrived, before, other, send_list, inv_alpha, vector, *outgoing):
    blocks = before.shape[1] // LANES
    ia = inv_alpha[0]

    def total(begin, size):
        rows = pl.ds(begin, size)
        return (arrived[0, rows, :] + arrived[1, rows, :]) + (
            arrived[2, rows, :] + arrived[3, rows, :]
        )

    vector[pl.ds(24, 8), :] = jnp.zeros((8, vector.shape[1]), F32)
    for block in range(blocks):
        lanes = pl.ds(block * LANES, LANES)
        weight = other[pl.ds(ROWS - 1, 1), lanes]
        for group in range(3):
            old = before[pl.ds(group * 8, 8), lanes]
            new = (weight * old + total((group * blocks + block) * 8, 8)) * ia - old
            vector[pl.ds(group * 8, 8), lanes] = new
        old = before[pl.ds(24, 1), lanes]
        new = (weight * old + total(24 * blocks + block, 1)) * ia - old
        vector[pl.ds(24, 1), lanes] = new

    def load(source, group):
        return vector[pl.ds(group * 8, 8), pl.ds(source * LANES, LANES)]

    for channel in range(4):
        index = send_list[:, pl.ds(channel * LANES, LANES)]
        for group, tile in enumerate(pick_lanes(index, (blocks, load), ROWS // 8)):
            outgoing[channel][pl.ds(group * 8, 8), :] = tile


def moment_kernel(v0, v1, v2, other, inv_alpha, moments):
    a, b, c = v0[...], v1[...], v2[...]
    weight = other[pl.ds(ROWS - 1, 1), :] * inv_alpha[0]
    group = [lane_sums(p) for p in (a * a, a * b, b * b, b * c, c * c, weight * (c * c))]
    moments[...] = 0.25 * jnp.concatenate(group + [jnp.zeros((2, LANES), F32)], axis=0)


def energy_kernel(*refs):
    vector, *ghosts = refs[:5]
    faces, mask, penalty = refs[5:8]
    coupling, inverse = refs[8:10], refs[10:12]
    scale, face_part, inv_alpha, moments = refs[12:16]
    weighted = refs[-1]
    gather_slots(vector, ghosts, faces, mask, weighted)
    w = weighted[...]
    s = scale[...]
    coupled = s * product(coupling, w)
    inside = product(inverse, coupled)
    if len(refs) == 18:
        refs[16][...] = s * inside
    local = lane_sums(coupled * inside) + lane_sums(penalty[...] * (w * w))
    row = lax.broadcasted_iota(jnp.int32, (8, LANES), 0)
    tile = face_part[...] + jnp.where(row == 5, local * inv_alpha[0], 0.0)
    for k in range(moments.shape[0]):
        moments[k] = tile


def sum_kernel(arrived, moments):
    total = arrived[0]
    for k in range(1, arrived.shape[0]):
        total = total + arrived[k]
    for k in range(moments.shape[0]):
        moments[k] = total


def weights_of(arrived, ia):
    total = arrived[0]
    for k in range(1, arrived.shape[0]):
        total = total + arrived[k]
    m = jnp.sum(total, axis=1, keepdims=True)
    m00, m01, m11, m12, m22, energy = (m[k : k + 1] for k in range(6))
    h00, h01, h02 = m00 + m01, m01 + m11, m11 + m12
    h11, h12, h22 = m11 + m12, m12 + m22, energy

    def inverse_of(pivot, whole):
        fine = pivot > 1e-7 * whole
        return jnp.where(fine, 1.0 / jnp.where(fine, pivot, 1.0), 0.0)

    i0 = inverse_of(h00, 0.0 * h00)
    l1, l2 = h01 * i0, h02 * i0
    i1 = inverse_of(h11 - l1 * h01, h11)
    e = h12 - l1 * h02
    l3 = e * i1
    i2 = inverse_of(h22 - l2 * h02 - l3 * e, h22)
    z1 = m01 - l1 * m00
    z2 = m11 - l2 * m00 - l3 * z1
    y2 = z2 * i2
    y1 = z1 * i1 - l3 * y2
    y0 = m00 * i0 - l1 * y1 - l2 * y2
    return y0 * ia, y1 * ia, y2 * ia


def second_kernel(*refs):
    arrived, v0, v1, v2, other = refs[:5]
    ghosts, inv_alpha, vector, outputs = refs[5:17], refs[17], refs[18], refs[19:]
    y0, y1, y2 = weights_of(arrived, inv_alpha[0])
    keep = lax.broadcasted_iota(jnp.int32, (ROWS, 1), 0) < ROWS - 1

    def start(explicit, a, b, c):
        weight = explicit[ROWS - 1 :]
        return jnp.where(keep, explicit, 0.0) + weight * (y0 * a + y1 * b + y2 * c)

    vector[...] = start(other[...], v0[...], v1[...], v2[...])
    for c in range(4):
        both = ghosts[c]
        outputs[c][...] = start(
            both[ROWS:, :], both[:ROWS, :], ghosts[4 + c][...], ghosts[8 + c][...]
        )


def trace_kernel(arrived, v0, v1, v2, inv_alpha, member, trace):
    y0, y1, y2 = weights_of(arrived, inv_alpha[0])
    nodes, owned = trace.shape
    mine = pl.ds(pl.multiple_of(member[0] * owned, LANES), owned)
    trace[...] = (y0 * v0[:, mine] + y1 * v1[:, mine] + y2 * v2[:, mine])[:nodes]


def interior_kernel(arrived, n0, n1, n2, inv_alpha, interior):
    y0, y1, y2 = weights_of(arrived, inv_alpha[0])
    interior[...] = y0 * n0[...] + y1 * n1[...] + y2 * n2[...]


def body(
    source_one,
    source_two,
    face_mass,
    penalty,
    interior_scale,
    coupling,
    inverse_block,
    element_faces,
    element_type,
    send_faces,
):
    members = lax.axis_size("sub")
    nodes, owned = source_one.shape
    group_width = members * owned
    elements = element_faces.shape[1]
    unknowns = coupling.shape[0]
    padded = -(-unknowns // LANES) * LANES
    reach = lax.axis_size(DOM) // 4
    domains = lax.axis_size(DOM)
    odd = lax.axis_index("core") % 2 == 1
    odd_far = lax.axis_index("zq") % 2 == 1

    pairs = (
        [(i, i + 1 if i % 2 == 0 else i - 1) for i in range(domains)],
        [(i, (i + 1 if i % 2 == 1 else i - 1) % domains) for i in range(domains)],
        [
            (i, (i + reach if (i // reach) % 2 == 0 else i - reach) % domains)
            for i in range(domains)
        ],
        [
            (i, (i + reach if (i // reach) % 2 == 1 else i - reach) % domains)
            for i in range(domains)
        ],
    )

    def exchange(payload):
        got = []
        for c in range(4):
            got.append(lax.ppermute(payload[c], DOM, pairs[c]))
        return got

    to_send = jnp.concatenate(
        [
            jnp.where(odd, send_faces[1], send_faces[0]),
            jnp.where(odd, send_faces[0], send_faces[1]),
            jnp.where(odd_far, send_faces[3], send_faces[2]),
            jnp.where(odd_far, send_faces[2], send_faces[3]),
        ]
    )
    near = element_faces - group_width
    direction = near // LANES
    swapped = jnp.where(direction < 2, jnp.where(odd, 0, 1), jnp.where(odd_far, 0, 1))
    remote = element_faces + LANES * jnp.where(
        swapped == 1, jnp.where(direction % 2 == 0, 1, -1), 0
    )
    faces = jnp.where(element_faces < group_width, element_faces, remote)
    faces = faces.reshape(1, -1)
    slots = faces.shape[1]
    spread = jnp.broadcast_to(faces.reshape(slots, 1), (slots, LANES))
    send_list = to_send.reshape(1, -1)
    send_spread = jnp.broadcast_to(to_send[:, None], (to_send.shape[0], LANES))
    mask = 1.0 - (element_type == 1).astype(F32)[None, :]
    weight = penalty[None, :]

    by_slot = coupling.reshape(unknowns, nodes, 6).transpose(0, 2, 1)
    by_slot = jnp.pad(by_slot, ((0, padded - unknowns), (0, 0), (0, ROWS - nodes)))
    by_slot = by_slot.reshape(padded, 6 * ROWS)
    extra = padded - unknowns
    padded_inverse = jnp.pad(inverse_block, ((0, extra), (0, extra)))
    lift, by_slot, inverse = (
        rounded_halves(m) for m in (by_slot.T, by_slot, padded_inverse)
    )
    scale = jnp.pad(interior_scale, ((0, extra), (0, 0)))

    spectrum = jnp.sum(coupling * jnp.dot(inverse_block, coupling)) / coupling.shape[1]
    inv_alpha = (1.0 / (0.6 + 2.4 * (1.1 + 1.35 * spectrum))).reshape(1)

    tile = shape(ROWS, LANES)
    mine = kernel_call(
        start_kernel, shape(members, 2 * ROWS, owned), source_one, source_two, face_mass[None, :]
    )
    everyone = lax.all_to_all(mine, "sub", 0, 0, tiled=True)
    v0, other, *outgoing = kernel_call(
        first_kernel,
        (shape(ROWS, group_width), shape(ROWS, group_width)) + (shape(2 * ROWS, LANES),) * 4,
        everyone,
        send_list,
    )
    start_ghosts = exchange(outgoing)
    member = lax.axis_index("sub").astype(jnp.int32).reshape(1)
    scratch = [pltpu.VMEM((6 * ROWS, elements), F32)]

    def apply(vector, ghosts, keep_inner):
        inner_shape = (shape(padded, elements),) if keep_inner else ()
        *returned, pieces = outs = kernel_call(
            apply_kernel,
            (tile,) * 4 + (shape(3 * ROWS, slots, dtype=BF16),) + inner_shape,
            vector,
            *ghosts,
            faces,
            spread,
            mask,
            weight,
            *by_slot,
            *lift,
            *inverse,
            scale,
            scratch=scratch,
        )
        returned, pieces, inner = outs[:4], outs[4], outs[5:]
        back = exchange(returned)
        placed = kernel_call(place_kernel, shape(ROWS, group_width), pieces, spread)
        packed = kernel_call(
            pack_kernel,
            shape(members, 24 * (group_width // LANES) + 24, LANES),
            placed,
            *back,
            send_spread,
        )
        arrived = lax.all_to_all(packed, "sub", 0, 0, tiled=True)
        following, *outgoing = kernel_call(
            next_kernel,
            (shape(ROWS, group_width),) + (tile,) * 4,
            arrived,
            vector,
            other,
            send_list,
            inv_alpha,
            specs=[VMEM] * 4 + [SMEM],
        )
        return following, exchange(outgoing), list(inner)

    count = 1
    for axis in NEAR:
        count *= lax.axis_size(axis)
    far = domains * members // count

    def section(v0, g0, keep_inner):
        inner_shape = (shape(padded, elements),) if keep_inner else ()
        v1, g1, n0 = apply(v0, g0, keep_inner)
        v2, g2, n1 = apply(v1, g1, keep_inner)
        face_part = kernel_call(
            moment_kernel, shape(8, LANES), v0, v1, v2, other, inv_alpha, specs=[VMEM] * 4 + [SMEM]
        )
        moments, *n2 = kernel_call(
            energy_kernel,
            (shape(count, 8, LANES),) + inner_shape,
            v2,
            *g2,
            faces,
            mask,
            weight,
            *by_slot,
            *inverse,
            scale,
            face_part,
            inv_alpha,
            specs=[VMEM] * 14 + [SMEM],
            scratch=scratch,
        )
        arrived = lax.all_to_all(moments, NEAR, 0, 0, tiled=True)
        moments = kernel_call(sum_kernel, shape(far, 8, LANES), arrived)
        arrived = lax.all_to_all(moments, FAR, 0, 0, tiled=True)
        return (v0, v1, v2), g1 + g2, n0 + n1 + n2, arrived

    vs, later_ghosts, _, arrived = section(v0, start_ghosts, False)
    u0, *h0 = kernel_call(
        second_kernel,
        (shape(ROWS, group_width),) + (tile,) * 4,
        arrived,
        *vs,
        other,
        *start_ghosts,
        *later_ghosts,
        inv_alpha,
        specs=[VMEM] * 17 + [SMEM],
    )
    vs, _, inners, arrived = section(u0, h0, True)
    trace_two = kernel_call(
        trace_kernel,
        shape(nodes, owned),
        arrived,
        *vs,
        inv_alpha,
        member,
        specs=[VMEM] * 4 + [SMEM] * 2,
    )
    rows = pl.BlockSpec((LANES, elements), lambda i: (i, 0))
    interior = pl.pallas_call(
        interior_kernel,
        out_shape=shape(unknowns, elements),
        grid=(padded // LANES,),
        in_specs=[pl.BlockSpec(arrived.shape, lambda i: (0, 0, 0))] + [rows] * 3 + [SMEM],
        out_specs=rows,
        name="interior",
        compiler_params=pltpu.CompilerParams(vmem_limit_bytes=16 << 20),
    )(arrived, *inners, inv_alpha)
    return trace_two, interior


def solution(mesh):
    sub = mesh.shape["sub"]
    split = Mesh(mesh.devices.reshape(4, 4, 4, 2, sub), ALL)
    return jax.shard_map(
        body,
        mesh=split,
        in_specs=(
            P(None, ALL),
            P(None, ALL),
            P(ALL),
            P(ALL),
            P(None, ALL),
            P(),
            P(),
            P(None, ALL),
            P(ALL),
            P(None, ALL),
        ),
        out_specs=(P(None, ALL), P(None, ALL)),
        check_vma=False,
    )
```

profile of v0, /device:TPU:24, one launch (start us, length us, event | category | flops | bytes accessed | tf_op | source)
XLA Modules:
  0.0 372.2 jit_solution(17156018989458935184)
XLA Ops:
  4.0 9.2 %all-to-all-start = ((f32[4,64,640]{2,1,0:T(8,128)}), f32[4,64,640]{2,1,0:T(8,128)S(1)}, u32[]{:S(2)}, u32[]{:S(2)}) async-start(f32[4,64,640]{2,1,0:T(8,128)} %shard_map.113), calls=%async_computation | async-start | bytes 1310720 | tf_op jit(solution)/shard_map/all_to_all | solution.py:409
  16.6 3.3 all-to-all-done.arrived
  20.6 1.9 collective-permute-start
  22.6 11.5 %collective-permute-start.1 = (f32[64,128]{1,0:T(8,128)S(1)}, f32[64,128]{1,0:T(8,128)S(1)}, u32[]{:S(2)}, u32[]{:S(2)}) collective-permute-start(f32[64,128]{1,0:T(8,128)S(1)} %get-tuple-element.59), channel_id=1, source_target_pairs={{0,508},{4,8},{8,4},{12,16},{16,12},{20,24},{24,20},{28,32},{32,28... | collective-permute-start | bytes 98312 | tf_op jit(solution)/shard_map/ppermute | solution.py:366
  34.0 1.9 collective-permute-start.2
  36.0 7.0 %collective-permute-start.3 = (f32[64,128]{1,0:T(8,128)S(1)}, f32[64,128]{1,0:T(8,128)S(1)}, u32[]{:S(2)}, u32[]{:S(2)}) collective-permute-start(f32[64,128]{1,0:T(8,128)S(1)} %get-tuple-element.61), channel_id=1, source_target_pairs={{0,384},{4,388},{8,392},{12,396},{16,400},{20,404},{24,408},{28,41... | collective-permute-start | bytes 98312 | tf_op jit(solution)/shard_map/ppermute | solution.py:366
  49.2 3.4 shard_map.115
  52.6 1.9 collective-permute-start.4
  54.6 4.6 %collective-permute-start.5 = (f32[32,128]{1,0:T(8,128)S(1)}, f32[32,128]{1,0:T(8,128)S(1)}, u32[]{:S(2)}, u32[]{:S(2)}) collective-permute-start(f32[32,128]{1,0:T(8,128)S(1)} %get-tuple-element.64), channel_id=1, source_target_pairs={{0,508},{4,8},{8,4},{12,16},{16,12},{20,24},{24,20},{28,32},{32,28... | collective-permute-start | bytes 49160 | tf_op jit(solution)/shard_map/ppermute | solution.py:366
  59.2 4.6 %collective-permute-start.6 = (f32[32,128]{1,0:T(8,128)S(1)}, f32[32,128]{1,0:T(8,128)S(1)}, u32[]{:S(2)}, u32[]{:S(2)}) collective-permute-start(f32[32,128]{1,0:T(8,128)S(1)} %get-tuple-element.65), channel_id=1, source_target_pairs={{0,128},{4,132},{8,136},{12,140},{16,144},{20,148},{24,152},{28,15... | collective-permute-start | bytes 49160 | tf_op jit(solution)/shard_map/ppermute | solution.py:366
  63.8 4.3 %collective-permute-start.7 = (f32[32,128]{1,0:T(8,128)S(1)}, f32[32,128]{1,0:T(8,128)S(1)}, u32[]{:S(2)}, u32[]{:S(2)}) collective-permute-start(f32[32,128]{1,0:T(8,128)S(1)} %get-tuple-element.66), channel_id=1, source_target_pairs={{0,384},{4,388},{8,392},{12,396},{16,400},{20,404},{24,408},{28,41... | collective-permute-start | bytes 49160 | tf_op jit(solution)/shard_map/ppermute | solution.py:366
  69.5 3.8 %collective-permute-done.7.r3 = f32[32,128]{1,0:T(8,128)S(1)} collective-permute-done((f32[32,128]{1,0:T(8,128)S(1)}, f32[32,128]{1,0:T(8,128)S(1)}, u32[]{:S(2)}, u32[]{:S(2)}) %collective-permute-start.7) | collective-permute-done | bytes 16416 | tf_op jit(solution)/shard_map/ppermute | solution.py:366
  75.1 6.3 %all-to-all-start.1 = ((f32[4,504,128]{2,1,0:T(8,128)}), f32[4,504,128]{2,1,0:T(8,128)}, u32[]{:S(2)}, u32[]{:S(2)}) async-start(f32[4,504,128]{2,1,0:T(8,128)} %copy-done.11), calls=%async_computation.1 | async-start | bytes 2064384 | tf_op jit(solution)/shard_map/all_to_all | solution.py:447
  81.4 2.3 fusion.1
  84.3 8.8 %all-to-all-done.1.arrived = f32[4,504,128]{2,1,0:T(8,128)} async-done(((f32[4,504,128]{2,1,0:T(8,128)}), f32[4,504,128]{2,1,0:T(8,128)}, u32[]{:S(2)}, u32[]{:S(2)}) %all-to-all-start.1) | async-done | bytes 1032224 | tf_op jit(solution)/shard_map/all_to_all | solution.py:447
  94.1 1.7 shard_map.118
  95.8 1.9 collective-permute-start.8
  97.8 5.5 %collective-permute-start.9 = (f32[32,128]{1,0:T(8,128)S(1)}, f32[32,128]{1,0:T(8,128)S(1)}, u32[]{:S(2)}, u32[]{:S(2)}) collective-permute-start(f32[32,128]{1,0:T(8,128)S(1)} %get-tuple-element.70), channel_id=1, source_target_pairs={{0,508},{4,8},{8,4},{12,16},{16,12},{20,24},{24,20},{28,32},{32,28... | collective-permute-start | bytes 49160 | tf_op jit(solution)/shard_map/ppermute | solution.py:366
  103.3 3.3 collective-permute-start.10
  106.6 5.7 %collective-permute-start.11 = (f32[32,128]{1,0:T(8,128)S(1)}, f32[32,128]{1,0:T(8,128)S(1)}, u32[]{:S(2)}, u32[]{:S(2)}) collective-permute-start(f32[32,128]{1,0:T(8,128)S(1)} %get-tuple-element.72), channel_id=1, source_target_pairs={{0,384},{4,388},{8,392},{12,396},{16,400},{20,404},{24,408},{28,41... | collective-permute-start | bytes 49160 | tf_op jit(solution)/shard_map/ppermute | solution.py:366
  112.8 3.3 collective-permute-done.11.refs_4_.refs_12_
  116.1 3.4 shard_map.119
  119.5 1.9 collective-permute-start.12
  121.5 3.6 collective-permute-start.13
  125.1 5.2 %collective-permute-start.14 = (f32[32,128]{1,0:T(8,128)S(1)}, f32[32,128]{1,0:T(8,128)S(1)}, u32[]{:S(2)}, u32[]{:S(2)}) collective-permute-start(f32[32,128]{1,0:T(8,128)S(1)} %get-tuple-element.76), channel_id=1, source_target_pairs={{0,128},{4,132},{8,136},{12,140},{16,144},{20,148},{24,152},{28,15... | collective-permute-start | bytes 49160 | tf_op jit(solution)/shard_map/ppermute | solution.py:366
  130.3 4.3 %collective-permute-start.15 = (f32[32,128]{1,0:T(8,128)S(1)}, f32[32,128]{1,0:T(8,128)S(1)}, u32[]{:S(2)}, u32[]{:S(2)}) collective-permute-start(f32[32,128]{1,0:T(8,128)S(1)} %get-tuple-element.77), channel_id=1, source_target_pairs={{0,384},{4,388},{8,392},{12,396},{16,400},{20,404},{24,408},{28,41... | collective-permute-start | bytes 49160 | tf_op jit(solution)/shard_map/ppermute | solution.py:366
  136.1 3.8 %collective-permute-done.15.r3 = f32[32,128]{1,0:T(8,128)S(1)} collective-permute-done((f32[32,128]{1,0:T(8,128)S(1)}, f32[32,128]{1,0:T(8,128)S(1)}, u32[]{:S(2)}, u32[]{:S(2)}) %collective-permute-start.15) | collective-permute-done | bytes 16416 | tf_op jit(solution)/shard_map/ppermute | solution.py:366
  140.5 16.4 %all_to_all.45.arrived = f32[4,504,128]{2,1,0:T(8,128)S(1)} all-to-all(f32[4,504,128]{2,1,0:T(8,128)S(1)} %shard_map.121), channel_id=1, replica_groups=mesh['zq'=4,'zr'=4,'x'=4,'core'=2,'sub'=4] {'sub'}, dimensions={0} | all-to-all | bytes 2064384 | tf_op jit(solution)/shard_map/all_to_all | solution.py:447
  157.3 1.9 collective-permute-start.16
  159.3 5.0 %collective-permute-start.17 = (f32[32,128]{1,0:T(8,128)S(1)}, f32[32,128]{1,0:T(8,128)S(1)}, u32[]{:S(2)}, u32[]{:S(2)}) collective-permute-start(f32[32,128]{1,0:T(8,128)S(1)} %get-tuple-element.80), channel_id=1, source_target_pairs={{0,508},{4,8},{8,4},{12,16},{16,12},{20,24},{24,20},{28,32},{32,28... | collective-permute-start | bytes 49160 | tf_op jit(solution)/shard_map/ppermute | solution.py:366
  164.2 2.3 collective-permute-start.18
  166.5 6.7 %collective-permute-start.19 = (f32[32,128]{1,0:T(8,128)S(1)}, f32[32,128]{1,0:T(8,128)S(1)}, u32[]{:S(2)}, u32[]{:S(2)}) collective-permute-start(f32[32,128]{1,0:T(8,128)S(1)} %get-tuple-element.82), channel_id=1, source_target_pairs={{0,384},{4,388},{8,392},{12,396},{16,400},{20,404},{24,408},{28,41... | collective-permute-start | bytes 49160 | tf_op jit(solution)/shard_map/ppermute | solution.py:366
  173.8 2.3 collective-permute-done.19.refs_4_.refs_16_
  176.0 2.7 shard_map.124
  178.7 11.0 %all_to_all.46.arrived = f32[32,8,128]{2,1,0:T(8,128)S(1)} all-to-all(f32[32,8,128]{2,1,0:T(8,128)S(1)} %shard_map.124), channel_id=1, replica_groups=mesh['zq'=4,'zr'=4,'x'=4,'core'=2,'sub'=4] {'x','core','sub'}, dimensions={0} | all-to-all | bytes 262144 | tf_op jit(solution)/shard_map/all_to_all | solution.py:488
  189.8 20.8 %all_to_all.47.refs_0_ = f32[16,8,128]{2,1,0:T(8,128)S(1)} all-to-all(f32[16,8,128]{2,1,0:T(8,128)S(1)} %shard_map.125), channel_id=1, replica_groups=mesh['zq'=4,'zr'=4,'x'=4,'core'=2,'sub'=4] {'zq','zr'}, dimensions={0} | all-to-all | bytes 131072 | tf_op jit(solution)/shard_map/all_to_all | solution.py:490
  211.0 3.4 shard_map.127
  215.3 1.9 collective-permute-start.20
  217.2 4.1 %collective-permute-start.21 = (f32[32,128]{1,0:T(8,128)S(1)}, f32[32,128]{1,0:T(8,128)S(1)}, u32[]{:S(2)}, u32[]{:S(2)}) collective-permute-start(f32[32,128]{1,0:T(8,128)S(1)} %get-tuple-element.90), channel_id=1, source_target_pairs={{0,508},{4,8},{8,4},{12,16},{16,12},{20,24},{24,20},{28,32},{32,28... | collective-permute-start | bytes 49160 | tf_op jit(solution)/shard_map/ppermute | solution.py:366
  221.3 4.3 %collective-permute-start.22 = (f32[32,128]{1,0:T(8,128)S(1)}, f32[32,128]{1,0:T(8,128)S(1)}, u32[]{:S(2)}, u32[]{:S(2)}) collective-permute-start(f32[32,128]{1,0:T(8,128)S(1)} %get-tuple-element.91), channel_id=1, source_target_pairs={{0,128},{4,132},{8,136},{12,140},{16,144},{20,148},{24,152},{28,15... | collective-permute-start | bytes 49160 | tf_op jit(solution)/shard_map/ppermute | solution.py:366
  225.6 2.9 collective-permute-start.23
  231.1 4.0 %collective-permute-done.23.r3 = f32[32,128]{1,0:T(8,128)S(1)} collective-permute-done((f32[32,128]{1,0:T(8,128)S(1)}, f32[32,128]{1,0:T(8,128)S(1)}, u32[]{:S(2)}, u32[]{:S(2)}) %collective-permute-start.23) | collective-permute-done | bytes 16416 | tf_op jit(solution)/shard_map/ppermute | solution.py:366
  235.7 13.9 %all_to_all.48.arrived = f32[4,504,128]{2,1,0:T(8,128)S(1)} all-to-all(f32[4,504,128]{2,1,0:T(8,128)S(1)} %shard_map.129), channel_id=1, replica_groups=mesh['zq'=4,'zr'=4,'x'=4,'core'=2,'sub'=4] {'sub'}, dimensions={0} | all-to-all | bytes 2064384 | tf_op jit(solution)/shard_map/all_to_all | solution.py:447
  250.1 1.9 collective-permute-start.24
  252.0 5.0 %collective-permute-start.25 = (f32[32,128]{1,0:T(8,128)S(1)}, f32[32,128]{1,0:T(8,128)S(1)}, u32[]{:S(2)}, u32[]{:S(2)}) collective-permute-start(f32[32,128]{1,0:T(8,128)S(1)} %get-tuple-element.95), channel_id=1, source_target_pairs={{0,508},{4,8},{8,4},{12,16},{16,12},{20,24},{24,20},{28,32},{32,28... | collective-permute-start | bytes 49160 | tf_op jit(solution)/shard_map/ppermute | solution.py:366
  257.1 4.6 %collective-permute-start.26 = (f32[32,128]{1,0:T(8,128)S(1)}, f32[32,128]{1,0:T(8,128)S(1)}, u32[]{:S(2)}, u32[]{:S(2)}) collective-permute-start(f32[32,128]{1,0:T(8,128)S(1)} %get-tuple-element.96), channel_id=1, source_target_pairs={{0,128},{4,132},{8,136},{12,140},{16,144},{20,148},{24,152},{28,15... | collective-permute-start | bytes 49160 | tf_op jit(solution)/shard_map/ppermute | solution.py:366
  261.7 7.0 %collective-permute-start.27 = (f32[32,128]{1,0:T(8,128)S(1)}, f32[32,128]{1,0:T(8,128)S(1)}, u32[]{:S(2)}, u32[]{:S(2)}) collective-permute-start(f32[32,128]{1,0:T(8,128)S(1)} %get-tuple-element.97), channel_id=1, source_target_pairs={{0,384},{4,388},{8,392},{12,396},{16,400},{20,404},{24,408},{28,41... | collective-permute-start | bytes 49160 | tf_op jit(solution)/shard_map/ppermute | solution.py:366
  268.7 2.5 collective-permute-done.27.refs_4_
  271.2 3.4 shard_map.131
  275.4 1.9 collective-permute-start.28
  277.4 5.7 %collective-permute-start.29 = (f32[32,128]{1,0:T(8,128)S(1)}, f32[32,128]{1,0:T(8,128)S(1)}, u32[]{:S(2)}, u32[]{:S(2)}) collective-permute-start(f32[32,128]{1,0:T(8,128)S(1)} %get-tuple-element.100), channel_id=1, source_target_pairs={{0,508},{4,8},{8,4},{12,16},{16,12},{20,24},{24,20},{28,32},{32,28... | collective-permute-start | bytes 49160 | tf_op jit(solution)/shard_map/ppermute | solution.py:366
  283.1 3.2 collective-permute-start.30
  286.3 6.5 %collective-permute-start.31 = (f32[32,128]{1,0:T(8,128)S(1)}, f32[32,128]{1,0:T(8,128)S(1)}, u32[]{:S(2)}, u32[]{:S(2)}) collective-permute-start(f32[32,128]{1,0:T(8,128)S(1)} %get-tuple-element.102), channel_id=1, source_target_pairs={{0,384},{4,388},{8,392},{12,396},{16,400},{20,404},{24,408},{28,41... | collective-permute-start | bytes 49160 | tf_op jit(solution)/shard_map/ppermute | solution.py:366
  296.4 16.1 %all_to_all.49.arrived = f32[4,504,128]{2,1,0:T(8,128)S(1)} all-to-all(f32[4,504,128]{2,1,0:T(8,128)S(1)} %shard_map.133), channel_id=1, replica_groups=mesh['zq'=4,'zr'=4,'x'=4,'core'=2,'sub'=4] {'sub'}, dimensions={0} | all-to-all | bytes 2064384 | tf_op jit(solution)/shard_map/all_to_all | solution.py:447
  313.0 1.9 collective-permute-start.32
  314.9 3.6 collective-permute-start.33
  318.5 6.0 %collective-permute-start.34 = (f32[32,128]{1,0:T(8,128)S(1)}, f32[32,128]{1,0:T(8,128)S(1)}, u32[]{:S(2)}, u32[]{:S(2)}) collective-permute-start(f32[32,128]{1,0:T(8,128)S(1)} %get-tuple-element.106), channel_id=1, source_target_pairs={{0,128},{4,132},{8,136},{12,140},{16,144},{20,148},{24,152},{28,15... | collective-permute-start | bytes 49160 | tf_op jit(solution)/shard_map/ppermute | solution.py:366
  324.5 4.8 %collective-permute-start.35 = (f32[32,128]{1,0:T(8,128)S(1)}, f32[32,128]{1,0:T(8,128)S(1)}, u32[]{:S(2)}, u32[]{:S(2)}) collective-permute-start(f32[32,128]{1,0:T(8,128)S(1)} %get-tuple-element.107), channel_id=1, source_target_pairs={{0,384},{4,388},{8,392},{12,396},{16,400},{20,404},{24,408},{28,41... | collective-permute-start | bytes 49160 | tf_op jit(solution)/shard_map/ppermute | solution.py:366
  329.6 4.4 %collective-permute-done.35.refs_4_ = f32[32,128]{1,0:T(8,128)S(1)} collective-permute-done((f32[32,128]{1,0:T(8,128)S(1)}, f32[32,128]{1,0:T(8,128)S(1)}, u32[]{:S(2)}, u32[]{:S(2)}) %collective-permute-start.35) | collective-permute-done | bytes 16416 | tf_op jit(solution)/shard_map/ppermute | solution.py:366
  334.1 2.7 shard_map.136
  336.8 11.1 %all_to_all.50.arrived = f32[32,8,128]{2,1,0:T(8,128)S(1)} all-to-all(f32[32,8,128]{2,1,0:T(8,128)S(1)} %get-tuple-element.108), channel_id=1, replica_groups=mesh['zq'=4,'zr'=4,'x'=4,'core'=2,'sub'=4] {'x','core','sub'}, dimensions={0} | all-to-all | bytes 262144 | tf_op jit(solution)/shard_map/all_to_all | solution.py:488
  348.6 7.7 %all-to-all-start.8 = ((f32[16,8,128]{2,1,0:T(8,128)}), f32[16,8,128]{2,1,0:T(8,128)S(1)}, u32[]{:S(2)}, u32[]{:S(2)}) async-start(f32[16,8,128]{2,1,0:T(8,128)} %shard_map.137), calls=%async_computation.8 | async-start | bytes 131072 | tf_op jit(solution)/shard_map/all_to_all | solution.py:490
  356.3 12.7 %all-to-all-done.8.arrived = f32[16,8,128]{2,1,0:T(8,128)S(1)} async-done(((f32[16,8,128]{2,1,0:T(8,128)}), f32[16,8,128]{2,1,0:T(8,128)S(1)}, u32[]{:S(2)}, u32[]{:S(2)}) %all-to-all-start.8) | async-done | bytes 65568 | tf_op jit(solution)/shard_map/all_to_all | solution.py:490
  370.3 1.9 interior.1
  (144 shorter events, 33.2 us)
Async XLA Ops:
  4.0 11.2 %copy-start.32 = (f32[500,150]{0,1:T(8,128)S(1)}, f32[500,150]{0,1:T(8,128)}, u32[]{:S(2)}) copy-start(f32[500,150]{0,1:T(8,128)} %param.15) | copy-start | bytes 900004
  4.0 15.9 %all-to-all-start = ((f32[4,64,640]{2,1,0:T(8,128)}), f32[4,64,640]{2,1,0:T(8,128)S(1)}, u32[]{:S(2)}, u32[]{:S(2)}) async-start(f32[4,64,640]{2,1,0:T(8,128)} %shard_map.113), calls=%async_computation | async-start | bytes 1310720 | tf_op jit(solution)/shard_map/all_to_all | solution.py:409
  20.6 27.9 %copy-start = (f32[32,2560]{1,0:T(8,128)}, f32[32,2560]{1,0:T(8,128)S(1)}, u32[]{:S(2)}) copy-start(f32[32,2560]{1,0:T(8,128)S(1)} %get-tuple-element.57.refs_0_.before.v0.refs_1_) | copy-start | bytes 983044
  20.6 25.1 %collective-permute-start = (f32[64,128]{1,0:T(8,128)S(1)}, f32[64,128]{1,0:T(8,128)S(1)}, u32[]{:S(2)}, u32[]{:S(2)}) collective-permute-start(f32[64,128]{1,0:T(8,128)S(1)} %get-tuple-element.58), channel_id=1, source_target_pairs={{0,4},{4,0},{8,12},{12,8},{16,20},{20,16},{24,28},{28,24},{32,36},... | collective-permute-start | bytes 98312 | tf_op jit(solution)/shard_map/ppermute | solution.py:366
  22.6 23.8 %collective-permute-start.1 = (f32[64,128]{1,0:T(8,128)S(1)}, f32[64,128]{1,0:T(8,128)S(1)}, u32[]{:S(2)}, u32[]{:S(2)}) collective-permute-start(f32[64,128]{1,0:T(8,128)S(1)} %get-tuple-element.59), channel_id=1, source_target_pairs={{0,508},{4,8},{8,4},{12,16},{16,12},{20,24},{24,20},{28,32},{32,28... | collective-permute-start | bytes 98312 | tf_op jit(solution)/shard_map/ppermute | solution.py:366
  34.0 12.9 %collective-permute-start.2 = (f32[64,128]{1,0:T(8,128)S(1)}, f32[64,128]{1,0:T(8,128)S(1)}, u32[]{:S(2)}, u32[]{:S(2)}) collective-permute-start(f32[64,128]{1,0:T(8,128)S(1)} %get-tuple-element.60), channel_id=1, source_target_pairs={{0,128},{4,132},{8,136},{12,140},{16,144},{20,148},{24,152},{28,15... | collective-permute-start | bytes 98312 | tf_op jit(solution)/shard_map/ppermute | solution.py:366
  36.0 9.7 %copy-start.33 = (f32[500,256]{1,0:T(8,128)S(1)}, f32[500,256]{1,0:T(8,128)}, u32[]{:S(2)}) copy-start(f32[500,256]{1,0:T(8,128)} %param.14) | copy-start | bytes 1536004
  36.0 11.6 %collective-permute-start.3 = (f32[64,128]{1,0:T(8,128)S(1)}, f32[64,128]{1,0:T(8,128)S(1)}, u32[]{:S(2)}, u32[]{:S(2)}) collective-permute-start(f32[64,128]{1,0:T(8,128)S(1)} %get-tuple-element.61), channel_id=1, source_target_pairs={{0,384},{4,388},{8,392},{12,396},{16,400},{20,404},{24,408},{28,41... | collective-permute-start | bytes 98312 | tf_op jit(solution)/shard_map/ppermute | solution.py:366
  45.7 2.5 copy-start.34
  48.2 1.0 copy-start.9
  48.2 1.0 copy-start.17
  48.2 1.0 copy-start.20
  48.2 1.0 copy-start.23
  48.2 1.0 copy-start.26
  52.6 16.9 %collective-permute-start.4 = (f32[32,128]{1,0:T(8,128)S(1)}, f32[32,128]{1,0:T(8,128)S(1)}, u32[]{:S(2)}, u32[]{:S(2)}) collective-permute-start(f32[32,128]{1,0:T(8,128)S(1)} %get-tuple-element.63), channel_id=1, source_target_pairs={{0,4},{4,0},{8,12},{12,8},{16,20},{20,16},{24,28},{28,24},{32,36},... | collective-permute-start | bytes 49160 | tf_op jit(solution)/shard_map/ppermute | solution.py:366
  54.6 14.9 %collective-permute-start.5 = (f32[32,128]{1,0:T(8,128)S(1)}, f32[32,128]{1,0:T(8,128)S(1)}, u32[]{:S(2)}, u32[]{:S(2)}) collective-permute-start(f32[32,128]{1,0:T(8,128)S(1)} %get-tuple-element.64), channel_id=1, source_target_pairs={{0,508},{4,8},{8,4},{12,16},{16,12},{20,24},{24,20},{28,32},{32,28... | collective-permute-start | bytes 49160 | tf_op jit(solution)/shard_map/ppermute | solution.py:366
  59.2 10.3 %collective-permute-start.6 = (f32[32,128]{1,0:T(8,128)S(1)}, f32[32,128]{1,0:T(8,128)S(1)}, u32[]{:S(2)}, u32[]{:S(2)}) collective-permute-start(f32[32,128]{1,0:T(8,128)S(1)} %get-tuple-element.65), channel_id=1, source_target_pairs={{0,128},{4,132},{8,136},{12,140},{16,144},{20,148},{24,152},{28,15... | collective-permute-start | bytes 49160 | tf_op jit(solution)/shard_map/ppermute | solution.py:366
  63.8 9.5 %collective-permute-start.7 = (f32[32,128]{1,0:T(8,128)S(1)}, f32[32,128]{1,0:T(8,128)S(1)}, u32[]{:S(2)}, u32[]{:S(2)}) collective-permute-start(f32[32,128]{1,0:T(8,128)S(1)} %get-tuple-element.66), channel_id=1, source_target_pairs={{0,384},{4,388},{8,392},{12,396},{16,400},{20,404},{24,408},{28,41... | collective-permute-start | bytes 49160 | tf_op jit(solution)/shard_map/ppermute | solution.py:366
  74.1 1.0 copy-start.11
  75.1 18.0 %all-to-all-start.1 = ((f32[4,504,128]{2,1,0:T(8,128)}), f32[4,504,128]{2,1,0:T(8,128)}, u32[]{:S(2)}, u32[]{:S(2)}) async-start(f32[4,504,128]{2,1,0:T(8,128)} %copy-done.11), calls=%async_computation.1 | async-start | bytes 2064384 | tf_op jit(solution)/shard_map/all_to_all | solution.py:447
  93.1 1.0 copy-start.1
  94.1 22.0 %copy-start.8 = (bf16[192,512]{1,0:T(8,128)(2,1)S(1)}, bf16[192,512]{1,0:T(8,128)(2,1)}, u32[]{:S(2)}) copy-start(bf16[192,512]{1,0:T(8,128)(2,1)} %get-tuple-element.116.refs_12_) | copy-start | bytes 589828
  94.1 22.0 %copy-start.10 = (bf16[192,512]{1,0:T(8,128)(2,1)S(1)}, bf16[192,512]{1,0:T(8,128)(2,1)}, u32[]{:S(2)}) copy-start(bf16[192,512]{1,0:T(8,128)(2,1)} %get-tuple-element.117.refs_11_) | copy-start | bytes 589828
  95.8 16.5 %collective-permute-start.8 = (f32[32,128]{1,0:T(8,128)S(1)}, f32[32,128]{1,0:T(8,128)S(1)}, u32[]{:S(2)}, u32[]{:S(2)}) collective-permute-start(f32[32,128]{1,0:T(8,128)S(1)} %get-tuple-element.69), channel_id=1, source_target_pairs={{0,4},{4,0},{8,12},{12,8},{16,20},{20,16},{24,28},{28,24},{32,36},... | collective-permute-start | bytes 49160 | tf_op jit(solution)/shard_map/ppermute | solution.py:366
  97.8 14.6 %collective-permute-start.9 = (f32[32,128]{1,0:T(8,128)S(1)}, f32[32,128]{1,0:T(8,128)S(1)}, u32[]{:S(2)}, u32[]{:S(2)}) collective-permute-start(f32[32,128]{1,0:T(8,128)S(1)} %get-tuple-element.70), channel_id=1, source_target_pairs={{0,508},{4,8},{8,4},{12,16},{16,12},{20,24},{24,20},{28,32},{32,28... | collective-permute-start | bytes 49160 | tf_op jit(solution)/shard_map/ppermute | solution.py:366
  103.3 9.5 %collective-permute-start.10 = (f32[32,128]{1,0:T(8,128)S(1)}, f32[32,128]{1,0:T(8,128)S(1)}, u32[]{:S(2)}, u32[]{:S(2)}) collective-permute-start(f32[32,128]{1,0:T(8,128)S(1)} %get-tuple-element.71), channel_id=1, source_target_pairs={{0,128},{4,132},{8,136},{12,140},{16,144},{20,148},{24,152},{28,15... | collective-permute-start | bytes 49160 | tf_op jit(solution)/shard_map/ppermute | solution.py:366
  106.6 9.6 %copy-start.31 = (f32[256]{0:T(256)S(1)}, f32[256]{0:T(256)}, u32[]{:S(2)}) copy-start(f32[256]{0:T(256)} %param.13) | copy-start | bytes 3076
  106.6 9.5 %collective-permute-start.11 = (f32[32,128]{1,0:T(8,128)S(1)}, f32[32,128]{1,0:T(8,128)S(1)}, u32[]{:S(2)}, u32[]{:S(2)}) collective-permute-start(f32[32,128]{1,0:T(8,128)S(1)} %get-tuple-element.72), channel_id=1, source_target_pairs={{0,384},{4,388},{8,392},{12,396},{16,400},{20,404},{24,408},{28,41... | collective-permute-start | bytes 49160 | tf_op jit(solution)/shard_map/ppermute | solution.py:366
  119.5 16.5 %collective-permute-start.12 = (f32[32,128]{1,0:T(8,128)S(1)}, f32[32,128]{1,0:T(8,128)S(1)}, u32[]{:S(2)}, u32[]{:S(2)}) collective-permute-start(f32[32,128]{1,0:T(8,128)S(1)} %get-tuple-element.74), channel_id=1, source_target_pairs={{0,4},{4,0},{8,12},{12,8},{16,20},{20,16},{24,28},{28,24},{32,36},... | collective-permute-start | bytes 49160 | tf_op jit(solution)/shard_map/ppermute | solution.py:366
  121.5 14.6 %collective-permute-start.13 = (f32[32,128]{1,0:T(8,128)S(1)}, f32[32,128]{1,0:T(8,128)S(1)}, u32[]{:S(2)}, u32[]{:S(2)}) collective-permute-start(f32[32,128]{1,0:T(8,128)S(1)} %get-tuple-element.75), channel_id=1, source_target_pairs={{0,508},{4,8},{8,4},{12,16},{16,12},{20,24},{24,20},{28,32},{32,28... | collective-permute-start | bytes 49160 | tf_op jit(solution)/shard_map/ppermute | solution.py:366
  125.1 11.0 %collective-permute-start.14 = (f32[32,128]{1,0:T(8,128)S(1)}, f32[32,128]{1,0:T(8,128)S(1)}, u32[]{:S(2)}, u32[]{:S(2)}) collective-permute-start(f32[32,128]{1,0:T(8,128)S(1)} %get-tuple-element.76), channel_id=1, source_target_pairs={{0,128},{4,132},{8,136},{12,140},{16,144},{20,148},{24,152},{28,15... | collective-permute-start | bytes 49160 | tf_op jit(solution)/shard_map/ppermute | solution.py:366
  130.3 9.5 %collective-permute-start.15 = (f32[32,128]{1,0:T(8,128)S(1)}, f32[32,128]{1,0:T(8,128)S(1)}, u32[]{:S(2)}, u32[]{:S(2)}) collective-permute-start(f32[32,128]{1,0:T(8,128)S(1)} %get-tuple-element.77), channel_id=1, source_target_pairs={{0,384},{4,388},{8,392},{12,396},{16,400},{20,404},{24,408},{28,41... | collective-permute-start | bytes 49160 | tf_op jit(solution)/shard_map/ppermute | solution.py:366
  156.9 16.3 %copy-start.2 = (f32[32,2560]{1,0:T(8,128)S(1)}, f32[32,2560]{1,0:T(8,128)}, u32[]{:S(2)}) copy-start(f32[32,2560]{1,0:T(8,128)} %copy-done) | copy-start | bytes 983044
  157.3 16.1 %collective-permute-start.16 = (f32[32,128]{1,0:T(8,128)S(1)}, f32[32,128]{1,0:T(8,128)S(1)}, u32[]{:S(2)}, u32[]{:S(2)}) collective-permute-start(f32[32,128]{1,0:T(8,128)S(1)} %get-tuple-element.79), channel_id=1, source_target_pairs={{0,4},{4,0},{8,12},{12,8},{16,20},{20,16},{24,28},{28,24},{32,36},... | collective-permute-start | bytes 49160 | tf_op jit(solution)/shard_map/ppermute | solution.py:366
  159.3 14.2 %collective-permute-start.17 = (f32[32,128]{1,0:T(8,128)S(1)}, f32[32,128]{1,0:T(8,128)S(1)}, u32[]{:S(2)}, u32[]{:S(2)}) collective-permute-start(f32[32,128]{1,0:T(8,128)S(1)} %get-tuple-element.80), channel_id=1, source_target_pairs={{0,508},{4,8},{8,4},{12,16},{16,12},{20,24},{24,20},{28,32},{32,28... | collective-permute-start | bytes 49160 | tf_op jit(solution)/shard_map/ppermute | solution.py:366
  164.2 9.5 %collective-permute-start.18 = (f32[32,128]{1,0:T(8,128)S(1)}, f32[32,128]{1,0:T(8,128)S(1)}, u32[]{:S(2)}, u32[]{:S(2)}) collective-permute-start(f32[32,128]{1,0:T(8,128)S(1)} %get-tuple-element.81), channel_id=1, source_target_pairs={{0,128},{4,132},{8,136},{12,140},{16,144},{20,148},{24,152},{28,15... | collective-permute-start | bytes 49160 | tf_op jit(solution)/shard_map/ppermute | solution.py:366
  166.5 9.5 %collective-permute-start.19 = (f32[32,128]{1,0:T(8,128)S(1)}, f32[32,128]{1,0:T(8,128)S(1)}, u32[]{:S(2)}, u32[]{:S(2)}) collective-permute-start(f32[32,128]{1,0:T(8,128)S(1)} %get-tuple-element.82), channel_id=1, source_target_pairs={{0,384},{4,388},{8,392},{12,396},{16,400},{20,404},{24,408},{28,41... | collective-permute-start | bytes 49160 | tf_op jit(solution)/shard_map/ppermute | solution.py:366
  189.8 20.9 %copy-start.18 = (f32[64,128]{1,0:T(8,128)S(1)}, f32[64,128]{1,0:T(8,128)}, u32[]{:S(2)}) copy-start(f32[64,128]{1,0:T(8,128)} %copy-done.16) | copy-start | bytes 98308
  189.8 20.8 %copy-start.21 = (f32[64,128]{1,0:T(8,128)S(1)}, f32[64,128]{1,0:T(8,128)}, u32[]{:S(2)}) copy-start(f32[64,128]{1,0:T(8,128)} %copy-done.19) | copy-start | bytes 98308
  189.8 20.8 %copy-start.24 = (f32[64,128]{1,0:T(8,128)S(1)}, f32[64,128]{1,0:T(8,128)}, u32[]{:S(2)}) copy-start(f32[64,128]{1,0:T(8,128)} %copy-done.22) | copy-start | bytes 98308
  189.8 20.8 %copy-start.27 = (f32[64,128]{1,0:T(8,128)S(1)}, f32[64,128]{1,0:T(8,128)}, u32[]{:S(2)}) copy-start(f32[64,128]{1,0:T(8,128)} %copy-done.25) | copy-start | bytes 98308
  211.0 118.4 %copy-start.3 = (f32[32,2560]{1,0:T(8,128)}, f32[32,2560]{1,0:T(8,128)S(1)}, u32[]{:S(2)}) copy-start(f32[32,2560]{1,0:T(8,128)S(1)} %get-tuple-element.83.refs_0_.before.v0) | copy-start | bytes 983044
  215.3 14.6 %collective-permute-start.20 = (f32[32,128]{1,0:T(8,128)S(1)}, f32[32,128]{1,0:T(8,128)S(1)}, u32[]{:S(2)}, u32[]{:S(2)}) collective-permute-start(f32[32,128]{1,0:T(8,128)S(1)} %get-tuple-element.89), channel_id=1, source_target_pairs={{0,4},{4,0},{8,12},{12,8},{16,20},{20,16},{24,28},{28,24},{32,36},... | collective-permute-start | bytes 49160 | tf_op jit(solution)/shard_map/ppermute | solution.py:366
  217.2 12.7 %collective-permute-start.21 = (f32[32,128]{1,0:T(8,128)S(1)}, f32[32,128]{1,0:T(8,128)S(1)}, u32[]{:S(2)}, u32[]{:S(2)}) collective-permute-start(f32[32,128]{1,0:T(8,128)S(1)} %get-tuple-element.90), channel_id=1, source_target_pairs={{0,508},{4,8},{8,4},{12,16},{16,12},{20,24},{24,20},{28,32},{32,28... | collective-permute-start | bytes 49160 | tf_op jit(solution)/shard_map/ppermute | solution.py:366
  221.3 9.8 %collective-permute-start.22 = (f32[32,128]{1,0:T(8,128)S(1)}, f32[32,128]{1,0:T(8,128)S(1)}, u32[]{:S(2)}, u32[]{:S(2)}) collective-permute-start(f32[32,128]{1,0:T(8,128)S(1)} %get-tuple-element.91), channel_id=1, source_target_pairs={{0,128},{4,132},{8,136},{12,140},{16,144},{20,148},{24,152},{28,15... | collective-permute-start | bytes 49160 | tf_op jit(solution)/shard_map/ppermute | solution.py:366
  225.6 9.5 %collective-permute-start.23 = (f32[32,128]{1,0:T(8,128)S(1)}, f32[32,128]{1,0:T(8,128)S(1)}, u32[]{:S(2)}, u32[]{:S(2)}) collective-permute-start(f32[32,128]{1,0:T(8,128)S(1)} %get-tuple-element.92), channel_id=1, source_target_pairs={{0,384},{4,388},{8,392},{12,396},{16,400},{20,404},{24,408},{28,41... | collective-permute-start | bytes 49160 | tf_op jit(solution)/shard_map/ppermute | solution.py:366
  250.1 79.2 %copy-start.5 = (f32[32,2560]{1,0:T(8,128)}, f32[32,2560]{1,0:T(8,128)S(1)}, u32[]{:S(2)}) copy-start(f32[32,2560]{1,0:T(8,128)S(1)} %get-tuple-element.93.refs_0_.before.v1) | copy-start | bytes 983044
  250.1 18.6 %collective-permute-start.24 = (f32[32,128]{1,0:T(8,128)S(1)}, f32[32,128]{1,0:T(8,128)S(1)}, u32[]{:S(2)}, u32[]{:S(2)}) collective-permute-start(f32[32,128]{1,0:T(8,128)S(1)} %get-tuple-element.94), channel_id=1, source_target_pairs={{0,4},{4,0},{8,12},{12,8},{16,20},{20,16},{24,28},{28,24},{32,36},... | collective-permute-start | bytes 49160 | tf_op jit(solution)/shard_map/ppermute | solution.py:366
  252.0 16.6 %collective-permute-start.25 = (f32[32,128]{1,0:T(8,128)S(1)}, f32[32,128]{1,0:T(8,128)S(1)}, u32[]{:S(2)}, u32[]{:S(2)}) collective-permute-start(f32[32,128]{1,0:T(8,128)S(1)} %get-tuple-element.95), channel_id=1, source_target_pairs={{0,508},{4,8},{8,4},{12,16},{16,12},{20,24},{24,20},{28,32},{32,28... | collective-permute-start | bytes 49160 | tf_op jit(solution)/shard_map/ppermute | solution.py:366
  257.1 11.6 %collective-permute-start.26 = (f32[32,128]{1,0:T(8,128)S(1)}, f32[32,128]{1,0:T(8,128)S(1)}, u32[]{:S(2)}, u32[]{:S(2)}) collective-permute-start(f32[32,128]{1,0:T(8,128)S(1)} %get-tuple-element.96), channel_id=1, source_target_pairs={{0,128},{4,132},{8,136},{12,140},{16,144},{20,148},{24,152},{28,15... | collective-permute-start | bytes 49160 | tf_op jit(solution)/shard_map/ppermute | solution.py:366
  261.7 9.5 %collective-permute-start.27 = (f32[32,128]{1,0:T(8,128)S(1)}, f32[32,128]{1,0:T(8,128)S(1)}, u32[]{:S(2)}, u32[]{:S(2)}) collective-permute-start(f32[32,128]{1,0:T(8,128)S(1)} %get-tuple-element.97), channel_id=1, source_target_pairs={{0,384},{4,388},{8,392},{12,396},{16,400},{20,404},{24,408},{28,41... | collective-permute-start | bytes 49160 | tf_op jit(solution)/shard_map/ppermute | solution.py:366
  275.4 18.7 %collective-permute-start.28 = (f32[32,128]{1,0:T(8,128)S(1)}, f32[32,128]{1,0:T(8,128)S(1)}, u32[]{:S(2)}, u32[]{:S(2)}) collective-permute-start(f32[32,128]{1,0:T(8,128)S(1)} %get-tuple-element.99), channel_id=1, source_target_pairs={{0,4},{4,0},{8,12},{12,8},{16,20},{20,16},{24,28},{28,24},{32,36},... | collective-permute-start | bytes 49160 | tf_op jit(solution)/shard_map/ppermute | solution.py:366
  277.4 16.8 %collective-permute-start.29 = (f32[32,128]{1,0:T(8,128)S(1)}, f32[32,128]{1,0:T(8,128)S(1)}, u32[]{:S(2)}, u32[]{:S(2)}) collective-permute-start(f32[32,128]{1,0:T(8,128)S(1)} %get-tuple-element.100), channel_id=1, source_target_pairs={{0,508},{4,8},{8,4},{12,16},{16,12},{20,24},{24,20},{28,32},{32,28... | collective-permute-start | bytes 49160 | tf_op jit(solution)/shard_map/ppermute | solution.py:366
  283.1 11.1 %collective-permute-start.30 = (f32[32,128]{1,0:T(8,128)S(1)}, f32[32,128]{1,0:T(8,128)S(1)}, u32[]{:S(2)}, u32[]{:S(2)}) collective-permute-start(f32[32,128]{1,0:T(8,128)S(1)} %get-tuple-element.101), channel_id=1, source_target_pairs={{0,128},{4,132},{8,136},{12,140},{16,144},{20,148},{24,152},{28,15... | collective-permute-start | bytes 49160 | tf_op jit(solution)/shard_map/ppermute | solution.py:366
  286.3 9.5 %collective-permute-start.31 = (f32[32,128]{1,0:T(8,128)S(1)}, f32[32,128]{1,0:T(8,128)S(1)}, u32[]{:S(2)}, u32[]{:S(2)}) collective-permute-start(f32[32,128]{1,0:T(8,128)S(1)} %get-tuple-element.102), channel_id=1, source_target_pairs={{0,384},{4,388},{8,392},{12,396},{16,400},{20,404},{24,408},{28,41... | collective-permute-start | bytes 49160 | tf_op jit(solution)/shard_map/ppermute | solution.py:366
  313.0 16.6 %collective-permute-start.32 = (f32[32,128]{1,0:T(8,128)S(1)}, f32[32,128]{1,0:T(8,128)S(1)}, u32[]{:S(2)}, u32[]{:S(2)}) collective-permute-start(f32[32,128]{1,0:T(8,128)S(1)} %get-tuple-element.104), channel_id=1, source_target_pairs={{0,4},{4,0},{8,12},{12,8},{16,20},{20,16},{24,28},{28,24},{32,36},... | collective-permute-start | bytes 49160 | tf_op jit(solution)/shard_map/ppermute | solution.py:366
  314.9 14.7 %collective-permute-start.33 = (f32[32,128]{1,0:T(8,128)S(1)}, f32[32,128]{1,0:T(8,128)S(1)}, u32[]{:S(2)}, u32[]{:S(2)}) collective-permute-start(f32[32,128]{1,0:T(8,128)S(1)} %get-tuple-element.105), channel_id=1, source_target_pairs={{0,508},{4,8},{8,4},{12,16},{16,12},{20,24},{24,20},{28,32},{32,28... | collective-permute-start | bytes 49160 | tf_op jit(solution)/shard_map/ppermute | solution.py:366
  318.5 11.1 %collective-permute-start.34 = (f32[32,128]{1,0:T(8,128)S(1)}, f32[32,128]{1,0:T(8,128)S(1)}, u32[]{:S(2)}, u32[]{:S(2)}) collective-permute-start(f32[32,128]{1,0:T(8,128)S(1)} %get-tuple-element.106), channel_id=1, source_target_pairs={{0,128},{4,132},{8,136},{12,140},{16,144},{20,148},{24,152},{28,15... | collective-permute-start | bytes 49160 | tf_op jit(solution)/shard_map/ppermute | solution.py:366
  324.5 9.6 %collective-permute-start.35 = (f32[32,128]{1,0:T(8,128)S(1)}, f32[32,128]{1,0:T(8,128)S(1)}, u32[]{:S(2)}, u32[]{:S(2)}) collective-permute-start(f32[32,128]{1,0:T(8,128)S(1)} %get-tuple-element.107), channel_id=1, source_target_pairs={{0,384},{4,388},{8,392},{12,396},{16,400},{20,404},{24,408},{28,41... | collective-permute-start | bytes 49160 | tf_op jit(solution)/shard_map/ppermute | solution.py:366
  334.1 35.0 %copy-start.6 = (f32[32,2560]{1,0:T(8,128)S(1)}, f32[32,2560]{1,0:T(8,128)}, u32[]{:S(2)}) copy-start(f32[32,2560]{1,0:T(8,128)} %copy-done.5) | copy-start | bytes 983044
  336.8 32.3 %copy-start.4 = (f32[32,2560]{1,0:T(8,128)S(1)}, f32[32,2560]{1,0:T(8,128)}, u32[]{:S(2)}) copy-start(f32[32,2560]{1,0:T(8,128)} %copy-done.3) | copy-start | bytes 983044
  348.6 20.5 %all-to-all-start.8 = ((f32[16,8,128]{2,1,0:T(8,128)}), f32[16,8,128]{2,1,0:T(8,128)S(1)}, u32[]{:S(2)}, u32[]{:S(2)}) async-start(f32[16,8,128]{2,1,0:T(8,128)} %shard_map.137), calls=%async_computation.8 | async-start | bytes 131072 | tf_op jit(solution)/shard_map/all_to_all | solution.py:490
  369.0 1.0 copy-start.13
  369.0 1.2 copy-start.15
  (14 other events, 10.3 us)
where the time goes:
time: 375 us; the launch traced here: 372 us
  starting transfers between devices  174 us (46%)
  blocking collectives  89.3 us (24%)
  waiting for transfers between devices  52.7 us (14%)
  Pallas kernels  36 us (10%)
  local copies, waits for them, and re-layouts  13.2 us (4%)
    ppermute x36, starting transfers between devices, exchange(): got.append(lax.ppermute(payload[c], DOM, pairs[c]))  150 us
    all_to_all x3, blocking collectives, apply(): arrived = lax.all_to_all(packed, 'sub', 0, 0, tiled=True)  46.4 us
    pallas_call x26, Pallas kernels, kernel_call(): pl.pallas_call(body, out_shape=outs, in_specs=specs or [VMEM] * len(args)...  34 us
    ppermute x36, waiting for transfers between devices, exchange(): got.append(lax.ppermute(payload[c], DOM, pairs[c]))  27.9 us
    all_to_all x2, blocking collectives, section(): arrived = lax.all_to_all(moments, NEAR, 0, 0, tiled=True)  22.1 us
    all_to_all x1, blocking collectives, section(): arrived = lax.all_to_all(moments, FAR, 0, 0, tiled=True)  20.8 us
    all_to_all x1, waiting for transfers between devices, section(): arrived = lax.all_to_all(moments, FAR, 0, 0, tiled=True)  12.7 us
    unnamed x80, local copies, waits for them, and re-layouts  11.3 us
  transfers between devices with their start and end apart: 39, of which 14 were waited for; matrix products, arithmetic and copies ran while one was open for 2% of the time, Pallas kernels for 2%

commit v1 on v0

--- a/solution.py
+++ b/solution.py
@@ -15,15 +15,17 @@
 NEAR = ("x", "core", "sub")
 FAR = ("zq", "zr")
 VMEM = pl.BlockSpec(memory_space=pltpu.VMEM)
+ANY = pl.BlockSpec(memory_space=pl.ANY)
+COPIED = pl.BlockSpec()
 SMEM = pl.BlockSpec(memory_space=pltpu.SMEM)
 
 
-def kernel_call(body, outs, *args, specs=None, scratch=()):
+def kernel_call(body, outs, *args, specs=None, out_specs=None, scratch=()):
     return pl.pallas_call(
         body,
         out_shape=outs,
         in_specs=specs or [VMEM] * len(args),
-        out_specs=jax.tree.map(lambda _: VMEM, outs),
+        out_specs=out_specs or jax.tree.map(lambda _: VMEM, outs),
         scratch_shapes=scratch,
         compiler_params=pltpu.CompilerParams(vmem_limit_bytes=32 << 20),
     )(*args)
@@ -100,7 +102,8 @@
         outgoing[member, 2 * ROWS - 1 :, :] = mass[...]
 
 
-def first_kernel(arrived, send_list, v0, other, *outgoing):
+def first_kernel(arrived, send_list, inv_alpha, v0, other, *outgoing):
+    del inv_alpha
     blocks = arrived.shape[2] // LANES
     for member in range(arrived.shape[0]):
         for block in range(blocks):
@@ -154,14 +157,18 @@
     faces, spread, mask, penalty = refs[5:9]
     coupling, lift, inverse = refs[9:11], refs[11:13], refs[13:15]
     scale = refs[15]
-    returned, pieces, weighted = refs[16:20], refs[20], refs[-1]
+    returned, pieces = refs[16:20], refs[20]
+    keep = len(refs) > 22
+    weighted = refs[22] if keep else refs[21]
     gather_slots(vector, ghosts, faces, mask, weighted)
     w = weighted[...]
     s = scale[...]
     coupled = s * product(coupling, w)
     inside = s * product(inverse, coupled)
-    if len(refs) == 23:
-        refs[21][...] = inside
+    if keep:
+        refs[23][...] = inside
+        leaving = pltpu.make_async_copy(refs[23], refs[21], refs[24])
+        leaving.start()
     contrib = penalty[...] * w + product(lift, inside)
     slots = [contrib[k * ROWS : (k + 1) * ROWS] for k in range(6)]
     slots[5] = slots[5] * mask[...]
@@ -174,6 +181,8 @@
         )
         returned[2 * pair][...] = onto[:, :LANES]
         returned[2 * pair + 1][...] = onto[:, LANES:]
+    if keep:
+        leaving.wait()
 
 
 def place_kernel(pieces, spread, placed):
@@ -312,16 +321,15 @@
         )
 
 
-def trace_kernel(arrived, v0, v1, v2, inv_alpha, member, trace):
-    y0, y1, y2 = weights_of(arrived, inv_alpha[0])
-    nodes, owned = trace.shape
-    mine = pl.ds(pl.multiple_of(member[0] * owned, LANES), owned)
-    trace[...] = (y0 * v0[:, mine] + y1 * v1[:, mine] + y2 * v2[:, mine])[:nodes]
-
-
-def interior_kernel(arrived, n0, n1, n2, inv_alpha, interior):
+def last_kernel(arrived, v0, v1, v2, n0, n1, n2, inv_alpha, member, trace, interior):
     y0, y1, y2 = weights_of(arrived, inv_alpha[0])
     interior[...] = y0 * n0[...] + y1 * n1[...] + y2 * n2[...]
+
+    @pl.when(pl.program_id(0) == 0)
+    def _():
+        nodes, owned = trace.shape
+        mine = pl.ds(pl.multiple_of(member[0] * owned, LANES), owned)
+        trace[...] = (y0 * v0[:, mine] + y1 * v1[:, mine] + y2 * v2[:, mine])[:nodes]
 
 
 def body(
@@ -404,7 +412,12 @@
 
     tile = shape(ROWS, LANES)
     mine = kernel_call(
-        start_kernel, shape(members, 2 * ROWS, owned), source_one, source_two, face_mass[None, :]
+        start_kernel,
+        shape(members, 2 * ROWS, owned),
+        source_one,
+        source_two,
+        face_mass[None, :],
+        specs=[COPIED] * 3,
     )
     everyone = lax.all_to_all(mine, "sub", 0, 0, tiled=True)
     v0, other, *outgoing = kernel_call(
@@ -412,14 +425,17 @@
         (shape(ROWS, group_width), shape(ROWS, group_width)) + (shape(2 * ROWS, LANES),) * 4,
         everyone,
         send_list,
+        inv_alpha,
+        specs=[VMEM, VMEM, SMEM],
     )
     start_ghosts = exchange(outgoing)
     member = lax.axis_index("sub").astype(jnp.int32).reshape(1)
     scratch = [pltpu.VMEM((6 * ROWS, elements), F32)]
+    copies = [pltpu.VMEM((padded, elements), F32), pltpu.SemaphoreType.DMA]
 
     def apply(vector, ghosts, keep_inner):
         inner_shape = (shape(padded, elements),) if keep_inner else ()
-        *returned, pieces = outs = kernel_call(
+        outs = kernel_call(
             apply_kernel,
             (tile,) * 4 + (shape(3 * ROWS, slots, dtype=BF16),) + inner_shape,
             vector,
@@ -432,7 +448,9 @@
             *lift,
             *inverse,
             scale,
-            scratch=scratch,
+            specs=[VMEM] + [COPIED if ghosts[0].shape[0] > ROWS else VMEM] * 4 + [VMEM] * 11,
+            out_specs=(VMEM,) * 5 + ((ANY,) if keep_inner else ()),
+            scratch=scratch + (copies if keep_inner else []),
         )
         returned, pieces, inner = outs[:4], outs[4], outs[5:]
         back = exchange(returned)
@@ -503,26 +521,16 @@
         specs=[VMEM] * 17 + [SMEM],
     )
     vs, _, inners, arrived = section(u0, h0, True)
-    trace_two = kernel_call(
-        trace_kernel,
-        shape(nodes, owned),
-        arrived,
-        *vs,
-        inv_alpha,
-        member,
-        specs=[VMEM] * 4 + [SMEM] * 2,
-    )
     rows = pl.BlockSpec((LANES, elements), lambda i: (i, 0))
-    interior = pl.pallas_call(
-        interior_kernel,
-        out_shape=shape(unknowns, elements),
+    return pl.pallas_call(
+        last_kernel,
+        out_shape=(shape(nodes, owned), shape(unknowns, elements)),
         grid=(padded // LANES,),
-        in_specs=[pl.BlockSpec(arrived.shape, lambda i: (0, 0, 0))] + [rows] * 3 + [SMEM],
-        out_specs=rows,
-        name="interior",
+        in_specs=[VMEM] * 4 + [rows] * 3 + [SMEM] * 2,
+        out_specs=(pl.BlockSpec((nodes, owned), lambda i: (0, 0)), rows),
+        name="last",
         compiler_params=pltpu.CompilerParams(vmem_limit_bytes=16 << 20),
-    )(arrived, *inners, inv_alpha)
-    return trace_two, interior
+    )(arrived, *vs, *inners, inv_alpha, member)
 
 
 def solution(mesh):

time: 375 us -> 368 us (0.981)
  blocking collectives: 89.3 us -> 106 us
  waiting for transfers between devices: 52.7 us -> 45 us
  starting transfers between devices: 174 us -> 168 us
  local copies, waits for them, and re-layouts: 13.2 us -> 8.29 us
    all_to_all x3 -> x4, blocking collectives: 46.4 us -> 62.5 us  [apply(): arrived = lax.all_to_all(packed, 'sub', 0, 0, tiled=True)]
    all_to_all x1 -> x0, waiting for transfers between devices: 8.82 us -> none  [apply(): arrived = lax.all_to_all(packed, 'sub', 0, 0, tiled=True)]
    all_to_all x1 -> x0, starting transfers between devices: 6.27 us -> none  [apply(): arrived = lax.all_to_all(packed, 'sub', 0, 0, tiled=True)]
    unnamed x80 -> x26, local copies, waits for them, and re-layouts: 11.3 us -> 5.88 us
    pallas_call x26 -> x25, Pallas kernels: 34 us -> 32.1 us  [kernel_call(): pl.pallas_call(body, out_shape=outs, in_specs=specs or [VMEM] * len(args)...]
  transfers between devices with their start and end apart: 39 -> 38, of which waited for: 14 -> 14; matrix products, arithmetic and copies ran while one was open for 2% -> 1% of each run, Pallas kernels for 2% -> 2%
where the time goes in v1:
time: 368 us; the launch traced here: 365 us
  starting transfers between devices  168 us (46%)
  blocking collectives  106 us (29%)
  waiting for transfers between devices  45 us (12%)
  Pallas kernels  34.1 us (9%)
  local copies, waits for them, and re-layouts  8.29 us (2%)
    ppermute x36, starting transfers between devices, exchange(): got.append(lax.ppermute(payload[c], DOM, pairs[c]))  151 us
    all_to_all x4, blocking collectives, apply(): arrived = lax.all_to_all(packed, 'sub', 0, 0, tiled=True)  62.5 us
    pallas_call x25, Pallas kernels, kernel_call(): pl.pallas_call(body, out_shape=outs, in_specs=specs or [VMEM] * len(args)...  32.1 us
    ppermute x36, waiting for transfers between devices, exchange(): got.append(lax.ppermute(payload[c], DOM, pairs[c]))  29.3 us
    all_to_all x2, blocking collectives, section(): arrived = lax.all_to_all(moments, NEAR, 0, 0, tiled=True)  22.1 us
    all_to_all x1, blocking collectives, section(): arrived = lax.all_to_all(moments, FAR, 0, 0, tiled=True)  21 us
    all_to_all x1, waiting for transfers between devices, section(): arrived = lax.all_to_all(moments, FAR, 0, 0, tiled=True)  12.7 us
    all_to_all x1, starting transfers between devices, body(): everyone = lax.all_to_all(mine, 'sub', 0, 0, tiled=True)  9.15 us
  transfers between devices with their start and end apart: 38, of which 14 were waited for; matrix products, arithmetic and copies ran while one was open for 1% of the time, Pallas kernels for 2%

profile of v1, /device:TPU:24, one launch (start us, length us, event | category | flops | bytes accessed | tf_op | source)
XLA Modules:
  0.0 365.4 jit_solution(7493237206181196496)
XLA Ops:
  4.0 9.2 %all-to-all-start = ((f32[4,64,640]{2,1,0:T(8,128)}), f32[4,64,640]{2,1,0:T(8,128)S(1)}, u32[]{:S(2)}, u32[]{:S(2)}) async-start(f32[4,64,640]{2,1,0:T(8,128)} %shard_map.113), calls=%async_computation | async-start | bytes 1310720 | tf_op jit(solution)/shard_map/all_to_all | solution.py:422
  16.9 2.9 all-to-all-done.arrived
  20.6 1.9 collective-permute-start
  22.6 11.5 %collective-permute-start.1 = (f32[64,128]{1,0:T(8,128)S(1)}, f32[64,128]{1,0:T(8,128)S(1)}, u32[]{:S(2)}, u32[]{:S(2)}) collective-permute-start(f32[64,128]{1,0:T(8,128)S(1)} %get-tuple-element.59), channel_id=1, source_target_pairs={{0,508},{4,8},{8,4},{12,16},{16,12},{20,24},{24,20},{28,32},{32,28... | collective-permute-start | bytes 98312 | tf_op jit(solution)/shard_map/ppermute | solution.py:374
  34.0 1.9 collective-permute-start.2
  36.0 6.9 %collective-permute-start.3 = (f32[64,128]{1,0:T(8,128)S(1)}, f32[64,128]{1,0:T(8,128)S(1)}, u32[]{:S(2)}, u32[]{:S(2)}) collective-permute-start(f32[64,128]{1,0:T(8,128)S(1)} %get-tuple-element.61), channel_id=1, source_target_pairs={{0,384},{4,388},{8,392},{12,396},{16,400},{20,404},{24,408},{28,41... | collective-permute-start | bytes 98312 | tf_op jit(solution)/shard_map/ppermute | solution.py:374
  42.9 1.4 fusion
  46.6 3.4 shard_map.115
  50.0 1.9 collective-permute-start.4
  52.0 6.4 %collective-permute-start.5 = (f32[32,128]{1,0:T(8,128)S(1)}, f32[32,128]{1,0:T(8,128)S(1)}, u32[]{:S(2)}, u32[]{:S(2)}) collective-permute-start(f32[32,128]{1,0:T(8,128)S(1)} %get-tuple-element.64), channel_id=1, source_target_pairs={{0,508},{4,8},{8,4},{12,16},{16,12},{20,24},{24,20},{28,32},{32,28... | collective-permute-start | bytes 49160 | tf_op jit(solution)/shard_map/ppermute | solution.py:374
  58.3 4.6 %collective-permute-start.6 = (f32[32,128]{1,0:T(8,128)S(1)}, f32[32,128]{1,0:T(8,128)S(1)}, u32[]{:S(2)}, u32[]{:S(2)}) collective-permute-start(f32[32,128]{1,0:T(8,128)S(1)} %get-tuple-element.65), channel_id=1, source_target_pairs={{0,128},{4,132},{8,136},{12,140},{16,144},{20,148},{24,152},{28,15... | collective-permute-start | bytes 49160 | tf_op jit(solution)/shard_map/ppermute | solution.py:374
  62.9 4.2 %collective-permute-start.7 = (f32[32,128]{1,0:T(8,128)S(1)}, f32[32,128]{1,0:T(8,128)S(1)}, u32[]{:S(2)}, u32[]{:S(2)}) collective-permute-start(f32[32,128]{1,0:T(8,128)S(1)} %get-tuple-element.66), channel_id=1, source_target_pairs={{0,384},{4,388},{8,392},{12,396},{16,400},{20,404},{24,408},{28,41... | collective-permute-start | bytes 49160 | tf_op jit(solution)/shard_map/ppermute | solution.py:374
  68.6 3.9 %collective-permute-done.7.r3 = f32[32,128]{1,0:T(8,128)S(1)} collective-permute-done((f32[32,128]{1,0:T(8,128)S(1)}, f32[32,128]{1,0:T(8,128)S(1)}, u32[]{:S(2)}, u32[]{:S(2)}) %collective-permute-start.7) | collective-permute-done | bytes 16416 | tf_op jit(solution)/shard_map/ppermute | solution.py:374
  73.2 15.6 %all_to_all.45.arrived = f32[4,504,128]{2,1,0:T(8,128)S(1)} all-to-all(f32[4,504,128]{2,1,0:T(8,128)S(1)} %shard_map.117), channel_id=1, replica_groups=mesh['zq'=4,'zr'=4,'x'=4,'core'=2,'sub'=4] {'sub'}, dimensions={0} | all-to-all | bytes 2064384 | tf_op jit(solution)/shard_map/all_to_all | solution.py:465
  89.3 1.9 collective-permute-start.8
  91.2 6.3 %collective-permute-start.9 = (f32[32,128]{1,0:T(8,128)S(1)}, f32[32,128]{1,0:T(8,128)S(1)}, u32[]{:S(2)}, u32[]{:S(2)}) collective-permute-start(f32[32,128]{1,0:T(8,128)S(1)} %get-tuple-element.70), channel_id=1, source_target_pairs={{0,508},{4,8},{8,4},{12,16},{16,12},{20,24},{24,20},{28,32},{32,28... | collective-permute-start | bytes 49160 | tf_op jit(solution)/shard_map/ppermute | solution.py:374
  97.6 2.4 collective-permute-start.10
  99.9 6.2 %collective-permute-start.11 = (f32[32,128]{1,0:T(8,128)S(1)}, f32[32,128]{1,0:T(8,128)S(1)}, u32[]{:S(2)}, u32[]{:S(2)}) collective-permute-start(f32[32,128]{1,0:T(8,128)S(1)} %get-tuple-element.72), channel_id=1, source_target_pairs={{0,384},{4,388},{8,392},{12,396},{16,400},{20,404},{24,408},{28,41... | collective-permute-start | bytes 49160 | tf_op jit(solution)/shard_map/ppermute | solution.py:374
  107.1 2.4 collective-permute-done.11.refs_4_.refs_12_
  109.5 3.4 shard_map.119
  112.9 1.9 collective-permute-start.12
  114.8 4.2 %collective-permute-start.13 = (f32[32,128]{1,0:T(8,128)S(1)}, f32[32,128]{1,0:T(8,128)S(1)}, u32[]{:S(2)}, u32[]{:S(2)}) collective-permute-start(f32[32,128]{1,0:T(8,128)S(1)} %get-tuple-element.75), channel_id=1, source_target_pairs={{0,508},{4,8},{8,4},{12,16},{16,12},{20,24},{24,20},{28,32},{32,28... | collective-permute-start | bytes 49160 | tf_op jit(solution)/shard_map/ppermute | solution.py:374
  119.0 5.1 %collective-permute-start.14 = (f32[32,128]{1,0:T(8,128)S(1)}, f32[32,128]{1,0:T(8,128)S(1)}, u32[]{:S(2)}, u32[]{:S(2)}) collective-permute-start(f32[32,128]{1,0:T(8,128)S(1)} %get-tuple-element.76), channel_id=1, source_target_pairs={{0,128},{4,132},{8,136},{12,140},{16,144},{20,148},{24,152},{28,15... | collective-permute-start | bytes 49160 | tf_op jit(solution)/shard_map/ppermute | solution.py:374
  124.1 3.1 collective-permute-start.15
  128.7 5.0 %collective-permute-done.15.r3 = f32[32,128]{1,0:T(8,128)S(1)} collective-permute-done((f32[32,128]{1,0:T(8,128)S(1)}, f32[32,128]{1,0:T(8,128)S(1)}, u32[]{:S(2)}, u32[]{:S(2)}) %collective-permute-start.15) | collective-permute-done | bytes 16416 | tf_op jit(solution)/shard_map/ppermute | solution.py:374
  134.3 16.8 %all_to_all.46.arrived = f32[4,504,128]{2,1,0:T(8,128)S(1)} all-to-all(f32[4,504,128]{2,1,0:T(8,128)S(1)} %shard_map.121), channel_id=1, replica_groups=mesh['zq'=4,'zr'=4,'x'=4,'core'=2,'sub'=4] {'sub'}, dimensions={0} | all-to-all | bytes 2064384 | tf_op jit(solution)/shard_map/all_to_all | solution.py:465
  151.6 1.9 collective-permute-start.16
  153.5 4.7 %collective-permute-start.17 = (f32[32,128]{1,0:T(8,128)S(1)}, f32[32,128]{1,0:T(8,128)S(1)}, u32[]{:S(2)}, u32[]{:S(2)}) collective-permute-start(f32[32,128]{1,0:T(8,128)S(1)} %get-tuple-element.80), channel_id=1, source_target_pairs={{0,508},{4,8},{8,4},{12,16},{16,12},{20,24},{24,20},{28,32},{32,28... | collective-permute-start | bytes 49160 | tf_op jit(solution)/shard_map/ppermute | solution.py:374
  158.2 2.1 collective-permute-start.18
  160.3 6.5 %collective-permute-start.19 = (f32[32,128]{1,0:T(8,128)S(1)}, f32[32,128]{1,0:T(8,128)S(1)}, u32[]{:S(2)}, u32[]{:S(2)}) collective-permute-start(f32[32,128]{1,0:T(8,128)S(1)} %get-tuple-element.82), channel_id=1, source_target_pairs={{0,384},{4,388},{8,392},{12,396},{16,400},{20,404},{24,408},{28,41... | collective-permute-start | bytes 49160 | tf_op jit(solution)/shard_map/ppermute | solution.py:374
  167.7 2.1 collective-permute-done.19.refs_4_.refs_16_
  169.9 2.7 shard_map.124
  172.6 11.0 %all_to_all.47.arrived = f32[32,8,128]{2,1,0:T(8,128)S(1)} all-to-all(f32[32,8,128]{2,1,0:T(8,128)S(1)} %shard_map.124), channel_id=1, replica_groups=mesh['zq'=4,'zr'=4,'x'=4,'core'=2,'sub'=4] {'x','core','sub'}, dimensions={0} | all-to-all | bytes 262144 | tf_op jit(solution)/shard_map/all_to_all | solution.py:506
  183.6 21.0 %all_to_all.48.refs_0_ = f32[16,8,128]{2,1,0:T(8,128)S(1)} all-to-all(f32[16,8,128]{2,1,0:T(8,128)S(1)} %shard_map.125), channel_id=1, replica_groups=mesh['zq'=4,'zr'=4,'x'=4,'core'=2,'sub'=4] {'zq','zr'}, dimensions={0} | all-to-all | bytes 131072 | tf_op jit(solution)/shard_map/all_to_all | solution.py:508
  204.9 3.5 shard_map.127
  208.5 1.9 collective-permute-start.20
  210.4 4.1 %collective-permute-start.21 = (f32[32,128]{1,0:T(8,128)S(1)}, f32[32,128]{1,0:T(8,128)S(1)}, u32[]{:S(2)}, u32[]{:S(2)}) collective-permute-start(f32[32,128]{1,0:T(8,128)S(1)} %get-tuple-element.90), channel_id=1, source_target_pairs={{0,508},{4,8},{8,4},{12,16},{16,12},{20,24},{24,20},{28,32},{32,28... | collective-permute-start | bytes 49160 | tf_op jit(solution)/shard_map/ppermute | solution.py:374
  214.5 4.3 %collective-permute-start.22 = (f32[32,128]{1,0:T(8,128)S(1)}, f32[32,128]{1,0:T(8,128)S(1)}, u32[]{:S(2)}, u32[]{:S(2)}) collective-permute-start(f32[32,128]{1,0:T(8,128)S(1)} %get-tuple-element.91), channel_id=1, source_target_pairs={{0,128},{4,132},{8,136},{12,140},{16,144},{20,148},{24,152},{28,15... | collective-permute-start | bytes 49160 | tf_op jit(solution)/shard_map/ppermute | solution.py:374
  218.8 2.9 collective-permute-start.23
  224.3 4.0 %collective-permute-done.23.r3 = f32[32,128]{1,0:T(8,128)S(1)} collective-permute-done((f32[32,128]{1,0:T(8,128)S(1)}, f32[32,128]{1,0:T(8,128)S(1)}, u32[]{:S(2)}, u32[]{:S(2)}) %collective-permute-start.23) | collective-permute-done | bytes 16416 | tf_op jit(solution)/shard_map/ppermute | solution.py:374
  229.0 13.9 %all_to_all.49.arrived = f32[4,504,128]{2,1,0:T(8,128)S(1)} all-to-all(f32[4,504,128]{2,1,0:T(8,128)S(1)} %shard_map.129), channel_id=1, replica_groups=mesh['zq'=4,'zr'=4,'x'=4,'core'=2,'sub'=4] {'sub'}, dimensions={0} | all-to-all | bytes 2064384 | tf_op jit(solution)/shard_map/all_to_all | solution.py:465
  243.3 1.9 collective-permute-start.24
  245.3 5.0 %collective-permute-start.25 = (f32[32,128]{1,0:T(8,128)S(1)}, f32[32,128]{1,0:T(8,128)S(1)}, u32[]{:S(2)}, u32[]{:S(2)}) collective-permute-start(f32[32,128]{1,0:T(8,128)S(1)} %get-tuple-element.95), channel_id=1, source_target_pairs={{0,508},{4,8},{8,4},{12,16},{16,12},{20,24},{24,20},{28,32},{32,28... | collective-permute-start | bytes 49160 | tf_op jit(solution)/shard_map/ppermute | solution.py:374
  250.3 4.6 %collective-permute-start.26 = (f32[32,128]{1,0:T(8,128)S(1)}, f32[32,128]{1,0:T(8,128)S(1)}, u32[]{:S(2)}, u32[]{:S(2)}) collective-permute-start(f32[32,128]{1,0:T(8,128)S(1)} %get-tuple-element.96), channel_id=1, source_target_pairs={{0,128},{4,132},{8,136},{12,140},{16,144},{20,148},{24,152},{28,15... | collective-permute-start | bytes 49160 | tf_op jit(solution)/shard_map/ppermute | solution.py:374
  254.9 7.0 %collective-permute-start.27 = (f32[32,128]{1,0:T(8,128)S(1)}, f32[32,128]{1,0:T(8,128)S(1)}, u32[]{:S(2)}, u32[]{:S(2)}) collective-permute-start(f32[32,128]{1,0:T(8,128)S(1)} %get-tuple-element.97), channel_id=1, source_target_pairs={{0,384},{4,388},{8,392},{12,396},{16,400},{20,404},{24,408},{28,41... | collective-permute-start | bytes 49160 | tf_op jit(solution)/shard_map/ppermute | solution.py:374
  261.9 2.5 collective-permute-done.27.refs_4_
  264.4 3.5 shard_map.131
  268.0 1.9 collective-permute-start.28
  269.9 5.7 %collective-permute-start.29 = (f32[32,128]{1,0:T(8,128)S(1)}, f32[32,128]{1,0:T(8,128)S(1)}, u32[]{:S(2)}, u32[]{:S(2)}) collective-permute-start(f32[32,128]{1,0:T(8,128)S(1)} %get-tuple-element.100), channel_id=1, source_target_pairs={{0,508},{4,8},{8,4},{12,16},{16,12},{20,24},{24,20},{28,32},{32,28... | collective-permute-start | bytes 49160 | tf_op jit(solution)/shard_map/ppermute | solution.py:374
  275.6 3.2 collective-permute-start.30
  278.9 6.4 %collective-permute-start.31 = (f32[32,128]{1,0:T(8,128)S(1)}, f32[32,128]{1,0:T(8,128)S(1)}, u32[]{:S(2)}, u32[]{:S(2)}) collective-permute-start(f32[32,128]{1,0:T(8,128)S(1)} %get-tuple-element.102), channel_id=1, source_target_pairs={{0,384},{4,388},{8,392},{12,396},{16,400},{20,404},{24,408},{28,41... | collective-permute-start | bytes 49160 | tf_op jit(solution)/shard_map/ppermute | solution.py:374
  285.3 1.4 shard_map.132.placed
  286.7 1.7 collective-permute-done.31.r3
  289.0 16.1 %all_to_all.50.arrived = f32[4,504,128]{2,1,0:T(8,128)S(1)} all-to-all(f32[4,504,128]{2,1,0:T(8,128)S(1)} %shard_map.133), channel_id=1, replica_groups=mesh['zq'=4,'zr'=4,'x'=4,'core'=2,'sub'=4] {'sub'}, dimensions={0} | all-to-all | bytes 2064384 | tf_op jit(solution)/shard_map/all_to_all | solution.py:465
  305.5 1.9 collective-permute-start.32
  307.5 3.6 collective-permute-start.33
  311.1 6.0 %collective-permute-start.34 = (f32[32,128]{1,0:T(8,128)S(1)}, f32[32,128]{1,0:T(8,128)S(1)}, u32[]{:S(2)}, u32[]{:S(2)}) collective-permute-start(f32[32,128]{1,0:T(8,128)S(1)} %get-tuple-element.106), channel_id=1, source_target_pairs={{0,128},{4,132},{8,136},{12,140},{16,144},{20,148},{24,152},{28,15... | collective-permute-start | bytes 49160 | tf_op jit(solution)/shard_map/ppermute | solution.py:374
  317.1 4.6 %collective-permute-start.35 = (f32[32,128]{1,0:T(8,128)S(1)}, f32[32,128]{1,0:T(8,128)S(1)}, u32[]{:S(2)}, u32[]{:S(2)}) collective-permute-start(f32[32,128]{1,0:T(8,128)S(1)} %get-tuple-element.107), channel_id=1, source_target_pairs={{0,384},{4,388},{8,392},{12,396},{16,400},{20,404},{24,408},{28,41... | collective-permute-start | bytes 49160 | tf_op jit(solution)/shard_map/ppermute | solution.py:374
  322.0 4.7 %collective-permute-done.35.refs_4_ = f32[32,128]{1,0:T(8,128)S(1)} collective-permute-done((f32[32,128]{1,0:T(8,128)S(1)}, f32[32,128]{1,0:T(8,128)S(1)}, u32[]{:S(2)}, u32[]{:S(2)}) %collective-permute-start.35) | collective-permute-done | bytes 16416 | tf_op jit(solution)/shard_map/ppermute | solution.py:374
  326.7 2.7 shard_map.136
  330.1 11.1 %all_to_all.51.arrived = f32[32,8,128]{2,1,0:T(8,128)S(1)} all-to-all(f32[32,8,128]{2,1,0:T(8,128)S(1)} %get-tuple-element.108), channel_id=1, replica_groups=mesh['zq'=4,'zr'=4,'x'=4,'core'=2,'sub'=4] {'x','core','sub'}, dimensions={0} | all-to-all | bytes 262144 | tf_op jit(solution)/shard_map/all_to_all | solution.py:506
  341.9 7.7 %all-to-all-start.8 = ((f32[16,8,128]{2,1,0:T(8,128)}), f32[16,8,128]{2,1,0:T(8,128)S(1)}, u32[]{:S(2)}, u32[]{:S(2)}) async-start(f32[16,8,128]{2,1,0:T(8,128)} %shard_map.137), calls=%async_computation.8 | async-start | bytes 131072 | tf_op jit(solution)/shard_map/all_to_all | solution.py:508
  349.6 12.7 %all-to-all-done.8.arrived = f32[16,8,128]{2,1,0:T(8,128)S(1)} async-done(((f32[16,8,128]{2,1,0:T(8,128)}), f32[16,8,128]{2,1,0:T(8,128)S(1)}, u32[]{:S(2)}, u32[]{:S(2)}) %all-to-all-start.8) | async-done | bytes 65568 | tf_op jit(solution)/shard_map/all_to_all | solution.py:508
  363.4 2.0 last.1
  (88 shorter events, 24.1 us)
Async XLA Ops:
  1.3 0.9 copy-start.4
  2.2 0.9 copy-start.5
  4.0 9.9 %copy-start.8 = (f32[500,150]{0,1:T(8,128)S(1)}, f32[500,150]{0,1:T(8,128)}, u32[]{:S(2)}) copy-start(f32[500,150]{0,1:T(8,128)} %param.15) | copy-start | bytes 900004
  4.0 10.0 %copy-start.7 = (f32[500,500]{1,0:T(8,128)S(1)}, f32[500,500]{1,0:T(8,128)}, u32[]{:S(2)}) copy-start(f32[500,500]{1,0:T(8,128)} %param.16) | copy-start | bytes 3000004
  4.0 15.9 %all-to-all-start = ((f32[4,64,640]{2,1,0:T(8,128)}), f32[4,64,640]{2,1,0:T(8,128)S(1)}, u32[]{:S(2)}, u32[]{:S(2)}) async-start(f32[4,64,640]{2,1,0:T(8,128)} %shard_map.113), calls=%async_computation | async-start | bytes 1310720 | tf_op jit(solution)/shard_map/all_to_all | solution.py:422
  13.2 0.7 copy-start.9
  14.0 1.0 copy-start.11
  15.0 0.7 copy-start.10
  20.6 24.7 %collective-permute-start = (f32[64,128]{1,0:T(8,128)S(1)}, f32[64,128]{1,0:T(8,128)S(1)}, u32[]{:S(2)}, u32[]{:S(2)}) collective-permute-start(f32[64,128]{1,0:T(8,128)S(1)} %get-tuple-element.58), channel_id=1, source_target_pairs={{0,4},{4,0},{8,12},{12,8},{16,20},{20,16},{24,28},{28,24},{32,36},... | collective-permute-start | bytes 98312 | tf_op jit(solution)/shard_map/ppermute | solution.py:374
  22.6 22.8 %collective-permute-start.1 = (f32[64,128]{1,0:T(8,128)S(1)}, f32[64,128]{1,0:T(8,128)S(1)}, u32[]{:S(2)}, u32[]{:S(2)}) collective-permute-start(f32[64,128]{1,0:T(8,128)S(1)} %get-tuple-element.59), channel_id=1, source_target_pairs={{0,508},{4,8},{8,4},{12,16},{16,12},{20,24},{24,20},{28,32},{32,28... | collective-permute-start | bytes 98312 | tf_op jit(solution)/shard_map/ppermute | solution.py:374
  34.0 11.3 %collective-permute-start.2 = (f32[64,128]{1,0:T(8,128)S(1)}, f32[64,128]{1,0:T(8,128)S(1)}, u32[]{:S(2)}, u32[]{:S(2)}) collective-permute-start(f32[64,128]{1,0:T(8,128)S(1)} %get-tuple-element.60), channel_id=1, source_target_pairs={{0,128},{4,132},{8,136},{12,140},{16,144},{20,148},{24,152},{28,15... | collective-permute-start | bytes 98312 | tf_op jit(solution)/shard_map/ppermute | solution.py:374
  36.0 9.7 %collective-permute-start.3 = (f32[64,128]{1,0:T(8,128)S(1)}, f32[64,128]{1,0:T(8,128)S(1)}, u32[]{:S(2)}, u32[]{:S(2)}) collective-permute-start(f32[64,128]{1,0:T(8,128)S(1)} %get-tuple-element.61), channel_id=1, source_target_pairs={{0,384},{4,388},{8,392},{12,396},{16,400},{20,404},{24,408},{28,41... | collective-permute-start | bytes 98312 | tf_op jit(solution)/shard_map/ppermute | solution.py:374
  45.9 0.7 copy-start.6
  50.0 18.5 %collective-permute-start.4 = (f32[32,128]{1,0:T(8,128)S(1)}, f32[32,128]{1,0:T(8,128)S(1)}, u32[]{:S(2)}, u32[]{:S(2)}) collective-permute-start(f32[32,128]{1,0:T(8,128)S(1)} %get-tuple-element.63), channel_id=1, source_target_pairs={{0,4},{4,0},{8,12},{12,8},{16,20},{20,16},{24,28},{28,24},{32,36},... | collective-permute-start | bytes 49160 | tf_op jit(solution)/shard_map/ppermute | solution.py:374
  52.0 16.6 %collective-permute-start.5 = (f32[32,128]{1,0:T(8,128)S(1)}, f32[32,128]{1,0:T(8,128)S(1)}, u32[]{:S(2)}, u32[]{:S(2)}) collective-permute-start(f32[32,128]{1,0:T(8,128)S(1)} %get-tuple-element.64), channel_id=1, source_target_pairs={{0,508},{4,8},{8,4},{12,16},{16,12},{20,24},{24,20},{28,32},{32,28... | collective-permute-start | bytes 49160 | tf_op jit(solution)/shard_map/ppermute | solution.py:374
  58.3 10.2 %collective-permute-start.6 = (f32[32,128]{1,0:T(8,128)S(1)}, f32[32,128]{1,0:T(8,128)S(1)}, u32[]{:S(2)}, u32[]{:S(2)}) collective-permute-start(f32[32,128]{1,0:T(8,128)S(1)} %get-tuple-element.65), channel_id=1, source_target_pairs={{0,128},{4,132},{8,136},{12,140},{16,144},{20,148},{24,152},{28,15... | collective-permute-start | bytes 49160 | tf_op jit(solution)/shard_map/ppermute | solution.py:374
  62.9 9.5 %collective-permute-start.7 = (f32[32,128]{1,0:T(8,128)S(1)}, f32[32,128]{1,0:T(8,128)S(1)}, u32[]{:S(2)}, u32[]{:S(2)}) collective-permute-start(f32[32,128]{1,0:T(8,128)S(1)} %get-tuple-element.66), channel_id=1, source_target_pairs={{0,384},{4,388},{8,392},{12,396},{16,400},{20,404},{24,408},{28,41... | collective-permute-start | bytes 49160 | tf_op jit(solution)/shard_map/ppermute | solution.py:374
  89.3 16.9 %collective-permute-start.8 = (f32[32,128]{1,0:T(8,128)S(1)}, f32[32,128]{1,0:T(8,128)S(1)}, u32[]{:S(2)}, u32[]{:S(2)}) collective-permute-start(f32[32,128]{1,0:T(8,128)S(1)} %get-tuple-element.69), channel_id=1, source_target_pairs={{0,4},{4,0},{8,12},{12,8},{16,20},{20,16},{24,28},{28,24},{32,36},... | collective-permute-start | bytes 49160 | tf_op jit(solution)/shard_map/ppermute | solution.py:374
  91.2 15.0 %collective-permute-start.9 = (f32[32,128]{1,0:T(8,128)S(1)}, f32[32,128]{1,0:T(8,128)S(1)}, u32[]{:S(2)}, u32[]{:S(2)}) collective-permute-start(f32[32,128]{1,0:T(8,128)S(1)} %get-tuple-element.70), channel_id=1, source_target_pairs={{0,508},{4,8},{8,4},{12,16},{16,12},{20,24},{24,20},{28,32},{32,28... | collective-permute-start | bytes 49160 | tf_op jit(solution)/shard_map/ppermute | solution.py:374
  97.6 9.5 %collective-permute-start.10 = (f32[32,128]{1,0:T(8,128)S(1)}, f32[32,128]{1,0:T(8,128)S(1)}, u32[]{:S(2)}, u32[]{:S(2)}) collective-permute-start(f32[32,128]{1,0:T(8,128)S(1)} %get-tuple-element.71), channel_id=1, source_target_pairs={{0,128},{4,132},{8,136},{12,140},{16,144},{20,148},{24,152},{28,15... | collective-permute-start | bytes 49160 | tf_op jit(solution)/shard_map/ppermute | solution.py:374
  99.9 9.5 %collective-permute-start.11 = (f32[32,128]{1,0:T(8,128)S(1)}, f32[32,128]{1,0:T(8,128)S(1)}, u32[]{:S(2)}, u32[]{:S(2)}) collective-permute-start(f32[32,128]{1,0:T(8,128)S(1)} %get-tuple-element.72), channel_id=1, source_target_pairs={{0,384},{4,388},{8,392},{12,396},{16,400},{20,404},{24,408},{28,41... | collective-permute-start | bytes 49160 | tf_op jit(solution)/shard_map/ppermute | solution.py:374
  112.9 15.8 %collective-permute-start.12 = (f32[32,128]{1,0:T(8,128)S(1)}, f32[32,128]{1,0:T(8,128)S(1)}, u32[]{:S(2)}, u32[]{:S(2)}) collective-permute-start(f32[32,128]{1,0:T(8,128)S(1)} %get-tuple-element.74), channel_id=1, source_target_pairs={{0,4},{4,0},{8,12},{12,8},{16,20},{20,16},{24,28},{28,24},{32,36},... | collective-permute-start | bytes 49160 | tf_op jit(solution)/shard_map/ppermute | solution.py:374
  114.8 13.9 %collective-permute-start.13 = (f32[32,128]{1,0:T(8,128)S(1)}, f32[32,128]{1,0:T(8,128)S(1)}, u32[]{:S(2)}, u32[]{:S(2)}) collective-permute-start(f32[32,128]{1,0:T(8,128)S(1)} %get-tuple-element.75), channel_id=1, source_target_pairs={{0,508},{4,8},{8,4},{12,16},{16,12},{20,24},{24,20},{28,32},{32,28... | collective-permute-start | bytes 49160 | tf_op jit(solution)/shard_map/ppermute | solution.py:374
  119.0 9.6 %collective-permute-start.14 = (f32[32,128]{1,0:T(8,128)S(1)}, f32[32,128]{1,0:T(8,128)S(1)}, u32[]{:S(2)}, u32[]{:S(2)}) collective-permute-start(f32[32,128]{1,0:T(8,128)S(1)} %get-tuple-element.76), channel_id=1, source_target_pairs={{0,128},{4,132},{8,136},{12,140},{16,144},{20,148},{24,152},{28,15... | collective-permute-start | bytes 49160 | tf_op jit(solution)/shard_map/ppermute | solution.py:374
  124.1 9.5 %collective-permute-start.15 = (f32[32,128]{1,0:T(8,128)S(1)}, f32[32,128]{1,0:T(8,128)S(1)}, u32[]{:S(2)}, u32[]{:S(2)}) collective-permute-start(f32[32,128]{1,0:T(8,128)S(1)} %get-tuple-element.77), channel_id=1, source_target_pairs={{0,384},{4,388},{8,392},{12,396},{16,400},{20,404},{24,408},{28,41... | collective-permute-start | bytes 49160 | tf_op jit(solution)/shard_map/ppermute | solution.py:374
  151.6 15.5 %collective-permute-start.16 = (f32[32,128]{1,0:T(8,128)S(1)}, f32[32,128]{1,0:T(8,128)S(1)}, u32[]{:S(2)}, u32[]{:S(2)}) collective-permute-start(f32[32,128]{1,0:T(8,128)S(1)} %get-tuple-element.79), channel_id=1, source_target_pairs={{0,4},{4,0},{8,12},{12,8},{16,20},{20,16},{24,28},{28,24},{32,36},... | collective-permute-start | bytes 49160 | tf_op jit(solution)/shard_map/ppermute | solution.py:374
  153.5 13.6 %collective-permute-start.17 = (f32[32,128]{1,0:T(8,128)S(1)}, f32[32,128]{1,0:T(8,128)S(1)}, u32[]{:S(2)}, u32[]{:S(2)}) collective-permute-start(f32[32,128]{1,0:T(8,128)S(1)} %get-tuple-element.80), channel_id=1, source_target_pairs={{0,508},{4,8},{8,4},{12,16},{16,12},{20,24},{24,20},{28,32},{32,28... | collective-permute-start | bytes 49160 | tf_op jit(solution)/shard_map/ppermute | solution.py:374
  158.2 9.5 %collective-permute-start.18 = (f32[32,128]{1,0:T(8,128)S(1)}, f32[32,128]{1,0:T(8,128)S(1)}, u32[]{:S(2)}, u32[]{:S(2)}) collective-permute-start(f32[32,128]{1,0:T(8,128)S(1)} %get-tuple-element.81), channel_id=1, source_target_pairs={{0,128},{4,132},{8,136},{12,140},{16,144},{20,148},{24,152},{28,15... | collective-permute-start | bytes 49160 | tf_op jit(solution)/shard_map/ppermute | solution.py:374
  160.3 9.5 %collective-permute-start.19 = (f32[32,128]{1,0:T(8,128)S(1)}, f32[32,128]{1,0:T(8,128)S(1)}, u32[]{:S(2)}, u32[]{:S(2)}) collective-permute-start(f32[32,128]{1,0:T(8,128)S(1)} %get-tuple-element.82), channel_id=1, source_target_pairs={{0,384},{4,388},{8,392},{12,396},{16,400},{20,404},{24,408},{28,41... | collective-permute-start | bytes 49160 | tf_op jit(solution)/shard_map/ppermute | solution.py:374
  208.5 14.6 %collective-permute-start.20 = (f32[32,128]{1,0:T(8,128)S(1)}, f32[32,128]{1,0:T(8,128)S(1)}, u32[]{:S(2)}, u32[]{:S(2)}) collective-permute-start(f32[32,128]{1,0:T(8,128)S(1)} %get-tuple-element.89), channel_id=1, source_target_pairs={{0,4},{4,0},{8,12},{12,8},{16,20},{20,16},{24,28},{28,24},{32,36},... | collective-permute-start | bytes 49160 | tf_op jit(solution)/shard_map/ppermute | solution.py:374
  210.4 12.7 %collective-permute-start.21 = (f32[32,128]{1,0:T(8,128)S(1)}, f32[32,128]{1,0:T(8,128)S(1)}, u32[]{:S(2)}, u32[]{:S(2)}) collective-permute-start(f32[32,128]{1,0:T(8,128)S(1)} %get-tuple-element.90), channel_id=1, source_target_pairs={{0,508},{4,8},{8,4},{12,16},{16,12},{20,24},{24,20},{28,32},{32,28... | collective-permute-start | bytes 49160 | tf_op jit(solution)/shard_map/ppermute | solution.py:374
  214.5 9.8 %collective-permute-start.22 = (f32[32,128]{1,0:T(8,128)S(1)}, f32[32,128]{1,0:T(8,128)S(1)}, u32[]{:S(2)}, u32[]{:S(2)}) collective-permute-start(f32[32,128]{1,0:T(8,128)S(1)} %get-tuple-element.91), channel_id=1, source_target_pairs={{0,128},{4,132},{8,136},{12,140},{16,144},{20,148},{24,152},{28,15... | collective-permute-start | bytes 49160 | tf_op jit(solution)/shard_map/ppermute | solution.py:374
  218.8 9.5 %collective-permute-start.23 = (f32[32,128]{1,0:T(8,128)S(1)}, f32[32,128]{1,0:T(8,128)S(1)}, u32[]{:S(2)}, u32[]{:S(2)}) collective-permute-start(f32[32,128]{1,0:T(8,128)S(1)} %get-tuple-element.92), channel_id=1, source_target_pairs={{0,384},{4,388},{8,392},{12,396},{16,400},{20,404},{24,408},{28,41... | collective-permute-start | bytes 49160 | tf_op jit(solution)/shard_map/ppermute | solution.py:374
  243.3 18.6 %collective-permute-start.24 = (f32[32,128]{1,0:T(8,128)S(1)}, f32[32,128]{1,0:T(8,128)S(1)}, u32[]{:S(2)}, u32[]{:S(2)}) collective-permute-start(f32[32,128]{1,0:T(8,128)S(1)} %get-tuple-element.94), channel_id=1, source_target_pairs={{0,4},{4,0},{8,12},{12,8},{16,20},{20,16},{24,28},{28,24},{32,36},... | collective-permute-start | bytes 49160 | tf_op jit(solution)/shard_map/ppermute | solution.py:374
  245.3 16.6 %collective-permute-start.25 = (f32[32,128]{1,0:T(8,128)S(1)}, f32[32,128]{1,0:T(8,128)S(1)}, u32[]{:S(2)}, u32[]{:S(2)}) collective-permute-start(f32[32,128]{1,0:T(8,128)S(1)} %get-tuple-element.95), channel_id=1, source_target_pairs={{0,508},{4,8},{8,4},{12,16},{16,12},{20,24},{24,20},{28,32},{32,28... | collective-permute-start | bytes 49160 | tf_op jit(solution)/shard_map/ppermute | solution.py:374
  250.3 11.6 %collective-permute-start.26 = (f32[32,128]{1,0:T(8,128)S(1)}, f32[32,128]{1,0:T(8,128)S(1)}, u32[]{:S(2)}, u32[]{:S(2)}) collective-permute-start(f32[32,128]{1,0:T(8,128)S(1)} %get-tuple-element.96), channel_id=1, source_target_pairs={{0,128},{4,132},{8,136},{12,140},{16,144},{20,148},{24,152},{28,15... | collective-permute-start | bytes 49160 | tf_op jit(solution)/shard_map/ppermute | solution.py:374
  254.9 9.5 %collective-permute-start.27 = (f32[32,128]{1,0:T(8,128)S(1)}, f32[32,128]{1,0:T(8,128)S(1)}, u32[]{:S(2)}, u32[]{:S(2)}) collective-permute-start(f32[32,128]{1,0:T(8,128)S(1)} %get-tuple-element.97), channel_id=1, source_target_pairs={{0,384},{4,388},{8,392},{12,396},{16,400},{20,404},{24,408},{28,41... | collective-permute-start | bytes 49160 | tf_op jit(solution)/shard_map/ppermute | solution.py:374
  268.0 18.7 %copy-start = (f32[512,256]{1,0:T(8,128)}, f32[512,256]{1,0:T(8,128)S(1)}, u32[]{:S(2)}) copy-start(f32[512,256]{1,0:T(8,128)S(1)} %get-tuple-element.110.n1) | copy-start | bytes 1572868
  268.0 18.7 %collective-permute-start.28 = (f32[32,128]{1,0:T(8,128)S(1)}, f32[32,128]{1,0:T(8,128)S(1)}, u32[]{:S(2)}, u32[]{:S(2)}) collective-permute-start(f32[32,128]{1,0:T(8,128)S(1)} %get-tuple-element.99), channel_id=1, source_target_pairs={{0,4},{4,0},{8,12},{12,8},{16,20},{20,16},{24,28},{28,24},{32,36},... | collective-permute-start | bytes 49160 | tf_op jit(solution)/shard_map/ppermute | solution.py:374
  269.9 16.8 %collective-permute-start.29 = (f32[32,128]{1,0:T(8,128)S(1)}, f32[32,128]{1,0:T(8,128)S(1)}, u32[]{:S(2)}, u32[]{:S(2)}) collective-permute-start(f32[32,128]{1,0:T(8,128)S(1)} %get-tuple-element.100), channel_id=1, source_target_pairs={{0,508},{4,8},{8,4},{12,16},{16,12},{20,24},{24,20},{28,32},{32,28... | collective-permute-start | bytes 49160 | tf_op jit(solution)/shard_map/ppermute | solution.py:374
  275.6 11.1 %collective-permute-start.30 = (f32[32,128]{1,0:T(8,128)S(1)}, f32[32,128]{1,0:T(8,128)S(1)}, u32[]{:S(2)}, u32[]{:S(2)}) collective-permute-start(f32[32,128]{1,0:T(8,128)S(1)} %get-tuple-element.101), channel_id=1, source_target_pairs={{0,128},{4,132},{8,136},{12,140},{16,144},{20,148},{24,152},{28,15... | collective-permute-start | bytes 49160 | tf_op jit(solution)/shard_map/ppermute | solution.py:374
  278.9 9.5 %collective-permute-start.31 = (f32[32,128]{1,0:T(8,128)S(1)}, f32[32,128]{1,0:T(8,128)S(1)}, u32[]{:S(2)}, u32[]{:S(2)}) collective-permute-start(f32[32,128]{1,0:T(8,128)S(1)} %get-tuple-element.102), channel_id=1, source_target_pairs={{0,384},{4,388},{8,392},{12,396},{16,400},{20,404},{24,408},{28,41... | collective-permute-start | bytes 49160 | tf_op jit(solution)/shard_map/ppermute | solution.py:374
  305.5 16.4 %collective-permute-start.32 = (f32[32,128]{1,0:T(8,128)S(1)}, f32[32,128]{1,0:T(8,128)S(1)}, u32[]{:S(2)}, u32[]{:S(2)}) collective-permute-start(f32[32,128]{1,0:T(8,128)S(1)} %get-tuple-element.104), channel_id=1, source_target_pairs={{0,4},{4,0},{8,12},{12,8},{16,20},{20,16},{24,28},{28,24},{32,36},... | collective-permute-start | bytes 49160 | tf_op jit(solution)/shard_map/ppermute | solution.py:374
  307.5 14.5 %collective-permute-start.33 = (f32[32,128]{1,0:T(8,128)S(1)}, f32[32,128]{1,0:T(8,128)S(1)}, u32[]{:S(2)}, u32[]{:S(2)}) collective-permute-start(f32[32,128]{1,0:T(8,128)S(1)} %get-tuple-element.105), channel_id=1, source_target_pairs={{0,508},{4,8},{8,4},{12,16},{16,12},{20,24},{24,20},{28,32},{32,28... | collective-permute-start | bytes 49160 | tf_op jit(solution)/shard_map/ppermute | solution.py:374
  311.1 10.9 %collective-permute-start.34 = (f32[32,128]{1,0:T(8,128)S(1)}, f32[32,128]{1,0:T(8,128)S(1)}, u32[]{:S(2)}, u32[]{:S(2)}) collective-permute-start(f32[32,128]{1,0:T(8,128)S(1)} %get-tuple-element.106), channel_id=1, source_target_pairs={{0,128},{4,132},{8,136},{12,140},{16,144},{20,148},{24,152},{28,15... | collective-permute-start | bytes 49160 | tf_op jit(solution)/shard_map/ppermute | solution.py:374
  317.1 9.6 %collective-permute-start.35 = (f32[32,128]{1,0:T(8,128)S(1)}, f32[32,128]{1,0:T(8,128)S(1)}, u32[]{:S(2)}, u32[]{:S(2)}) collective-permute-start(f32[32,128]{1,0:T(8,128)S(1)} %get-tuple-element.107), channel_id=1, source_target_pairs={{0,384},{4,388},{8,392},{12,396},{16,400},{20,404},{24,408},{28,41... | collective-permute-start | bytes 49160 | tf_op jit(solution)/shard_map/ppermute | solution.py:374
  329.3 0.8 copy-start.2
  330.1 32.2 %copy-start.1 = (f32[512,256]{1,0:T(8,128)S(1)}, f32[512,256]{1,0:T(8,128)}, u32[]{:S(2)}) copy-start(f32[512,256]{1,0:T(8,128)} %copy-done) | copy-start | bytes 1572868
  341.9 20.4 %all-to-all-start.8 = ((f32[16,8,128]{2,1,0:T(8,128)}), f32[16,8,128]{2,1,0:T(8,128)S(1)}, u32[]{:S(2)}, u32[]{:S(2)}) async-start(f32[16,8,128]{2,1,0:T(8,128)} %shard_map.137), calls=%async_computation.8 | async-start | bytes 131072 | tf_op jit(solution)/shard_map/all_to_all | solution.py:508
  362.4 1.0 copy-start.3

commit v2 on v1

--- a/solution.py
+++ b/solution.py
@@ -92,18 +92,29 @@
     return jnp.sum(total, axis=0, keepdims=True)
 
 
-def start_kernel(one, two, mass, outgoing):
+def start_kernel(one, two, mass, outgoing, near_one, near_two, near_mass, ready):
+    copies = [
+        pltpu.make_async_copy(source, target, ready.at[k])
+        for k, (source, target) in enumerate(
+            ((one, near_one), (two, near_two), (mass, near_mass))
+        )
+    ]
+    for copy in copies:
+        copy.start()
     nodes, owned = one.shape
     for member in range(outgoing.shape[0]):
-        outgoing[member, :nodes, :] = one[...]
         outgoing[member, nodes:ROWS, :] = jnp.zeros((ROWS - nodes, owned), F32)
-        outgoing[member, ROWS : ROWS + nodes, :] = two[...]
         outgoing[member, ROWS + nodes : 2 * ROWS - 1, :] = jnp.zeros((ROWS - 1 - nodes, owned), F32)
-        outgoing[member, 2 * ROWS - 1 :, :] = mass[...]
-
-
-def first_kernel(arrived, send_list, inv_alpha, v0, other, *outgoing):
-    del inv_alpha
+    for copy in copies:
+        copy.wait()
+    for member in range(outgoing.shape[0]):
+        outgoing[member, :nodes, :] = near_one[...]
+        outgoing[member, ROWS : ROWS + nodes, :] = near_two[...]
+        outgoing[member, 2 * ROWS - 1 :, :] = near_mass[...].reshape(1, owned)
+
+
+def first_kernel(arrived, send_list, *refs):
+    v0, other, *outgoing = refs[-6:]
     blocks = arrived.shape[2] // LANES
     for member in range(arrived.shape[0]):
         for block in range(blocks):
@@ -321,15 +332,13 @@
         )
 
 
-def last_kernel(arrived, v0, v1, v2, n0, n1, n2, inv_alpha, member, trace, interior):
+def last_kernel(arrived, v0, v1, v2, inv_alpha, member, trace, weights):
     y0, y1, y2 = weights_of(arrived, inv_alpha[0])
-    interior[...] = y0 * n0[...] + y1 * n1[...] + y2 * n2[...]
-
-    @pl.when(pl.program_id(0) == 0)
-    def _():
-        nodes, owned = trace.shape
-        mine = pl.ds(pl.multiple_of(member[0] * owned, LANES), owned)
-        trace[...] = (y0 * v0[:, mine] + y1 * v1[:, mine] + y2 * v2[:, mine])[:nodes]
+    nodes, owned = trace.shape
+    mine = pl.ds(pl.multiple_of(member[0] * owned, LANES), owned)
+    trace[...] = (y0 * v0[:, mine] + y1 * v1[:, mine] + y2 * v2[:, mine])[:nodes]
+    for k, y in enumerate((y0, y1, y2)):
+        weights[k : k + 1, :] = jnp.broadcast_to(y, (1, weights.shape[1]))
 
 
 def body(
@@ -416,17 +425,24 @@
         shape(members, 2 * ROWS, owned),
         source_one,
         source_two,
-        face_mass[None, :],
-        specs=[COPIED] * 3,
-    )
+        face_mass,
+        specs=[ANY] * 3,
+        scratch=[
+            pltpu.VMEM((nodes, owned), F32),
+            pltpu.VMEM((nodes, owned), F32),
+            pltpu.VMEM((owned,), F32),
+            pltpu.SemaphoreType.DMA((3,)),
+        ],
+    )
+    early = (inv_alpha, *by_slot, *lift, *inverse, scale, spread, send_spread, mask, faces)
     everyone = lax.all_to_all(mine, "sub", 0, 0, tiled=True)
     v0, other, *outgoing = kernel_call(
         first_kernel,
         (shape(ROWS, group_width), shape(ROWS, group_width)) + (shape(2 * ROWS, LANES),) * 4,
         everyone,
         send_list,
-        inv_alpha,
-        specs=[VMEM, VMEM, SMEM],
+        *early,
+        specs=[VMEM, VMEM] + [ANY] * len(early),
     )
     start_ghosts = exchange(outgoing)
     member = lax.axis_index("sub").astype(jnp.int32).reshape(1)
@@ -521,16 +537,17 @@
         specs=[VMEM] * 17 + [SMEM],
     )
     vs, _, inners, arrived = section(u0, h0, True)
-    rows = pl.BlockSpec((LANES, elements), lambda i: (i, 0))
-    return pl.pallas_call(
+    trace_two, weights = kernel_call(
         last_kernel,
-        out_shape=(shape(nodes, owned), shape(unknowns, elements)),
-        grid=(padded // LANES,),
-        in_specs=[VMEM] * 4 + [rows] * 3 + [SMEM] * 2,
-        out_specs=(pl.BlockSpec((nodes, owned), lambda i: (0, 0)), rows),
-        name="last",
-        compiler_params=pltpu.CompilerParams(vmem_limit_bytes=16 << 20),
-    )(arrived, *vs, *inners, inv_alpha, member)
+        (shape(nodes, owned), shape(3, elements)),
+        arrived,
+        *vs,
+        inv_alpha,
+        member,
+        specs=[VMEM] * 4 + [SMEM] * 2,
+    )
+    interior = sum(weights[k][None, :] * inners[k][:unknowns] for k in range(3))
+    return trace_two, interior
 
 
 def solution(mesh):

time: 368 us -> 368 us (level)
    unnamed x26 -> x36, local copies, waits for them, and re-layouts: 5.88 us -> 8.39 us
    pallas_call x25 -> x26, Pallas kernels: 32.1 us -> 33.2 us  [kernel_call(): pl.pallas_call(body, out_shape=outs, in_specs=specs or [VMEM] * len(args)...]
where the time goes in v2:
time: 368 us; the launch traced here: 365 us
  starting transfers between devices  167 us (45%)
  blocking collectives  106 us (29%)
  waiting for transfers between devices  44.4 us (12%)
  Pallas kernels  33.2 us (9%)
  local copies, waits for them, and re-layouts  9.9 us (3%)
    ppermute x36, starting transfers between devices, exchange(): got.append(lax.ppermute(payload[c], DOM, pairs[c]))  151 us
    all_to_all x4, blocking collectives, apply(): arrived = lax.all_to_all(packed, 'sub', 0, 0, tiled=True)  62.5 us
    pallas_call x26, Pallas kernels, kernel_call(): pl.pallas_call(body, out_shape=outs, in_specs=specs or [VMEM] * len(args)...  33.2 us
    ppermute x36, waiting for transfers between devices, exchange(): got.append(lax.ppermute(payload[c], DOM, pairs[c]))  31.6 us
    all_to_all x2, blocking collectives, section(): arrived = lax.all_to_all(moments, NEAR, 0, 0, tiled=True)  22.1 us
    all_to_all x1, blocking collectives, section(): arrived = lax.all_to_all(moments, FAR, 0, 0, tiled=True)  20.9 us
    all_to_all x1, waiting for transfers between devices, section(): arrived = lax.all_to_all(moments, FAR, 0, 0, tiled=True)  12.7 us
    all_to_all x1, starting transfers between devices, body(): everyone = lax.all_to_all(mine, 'sub', 0, 0, tiled=True)  9.16 us
  transfers between devices with their start and end apart: 38, of which 14 were waited for; matrix products, arithmetic and copies ran while one was open for 1% of the time, Pallas kernels for 2%

profile of v2, /device:TPU:24, one launch (start us, length us, event | category | flops | bytes accessed | tf_op | source)
XLA Modules:
  0.0 364.8 jit_solution(16184438378802943934)
XLA Ops:
  4.3 9.2 %all-to-all-start = ((f32[4,64,640]{2,1,0:T(8,128)}), f32[4,64,640]{2,1,0:T(8,128)S(1)}, u32[]{:S(2)}, u32[]{:S(2)}) async-start(f32[4,64,640]{2,1,0:T(8,128)} %shard_map.113), calls=%async_computation | async-start | bytes 1310720 | tf_op jit(solution)/shard_map/all_to_all | solution.py:438
  21.9 1.9 collective-permute-start
  23.8 10.9 %collective-permute-start.1 = (f32[64,128]{1,0:T(8,128)S(1)}, f32[64,128]{1,0:T(8,128)S(1)}, u32[]{:S(2)}, u32[]{:S(2)}) collective-permute-start(f32[64,128]{1,0:T(8,128)S(1)} %get-tuple-element.61), channel_id=1, source_target_pairs={{0,508},{4,8},{8,4},{12,16},{16,12},{20,24},{24,20},{28,32},{32,28... | collective-permute-start | bytes 98312 | tf_op jit(solution)/shard_map/ppermute | solution.py:383
  34.7 1.9 collective-permute-start.2
  36.7 6.9 %collective-permute-start.3 = (f32[64,128]{1,0:T(8,128)S(1)}, f32[64,128]{1,0:T(8,128)S(1)}, u32[]{:S(2)}, u32[]{:S(2)}) collective-permute-start(f32[64,128]{1,0:T(8,128)S(1)} %get-tuple-element.63), channel_id=1, source_target_pairs={{0,384},{4,388},{8,392},{12,396},{16,400},{20,404},{24,408},{28,41... | collective-permute-start | bytes 98312 | tf_op jit(solution)/shard_map/ppermute | solution.py:383
  44.5 1.8 collective-permute-done.3.refs_4_.refs_8_
  47.0 3.4 shard_map.115
  50.5 1.9 collective-permute-start.4
  52.4 6.4 %collective-permute-start.5 = (f32[32,128]{1,0:T(8,128)S(1)}, f32[32,128]{1,0:T(8,128)S(1)}, u32[]{:S(2)}, u32[]{:S(2)}) collective-permute-start(f32[32,128]{1,0:T(8,128)S(1)} %get-tuple-element.66), channel_id=1, source_target_pairs={{0,508},{4,8},{8,4},{12,16},{16,12},{20,24},{24,20},{28,32},{32,28... | collective-permute-start | bytes 49160 | tf_op jit(solution)/shard_map/ppermute | solution.py:383
  58.8 4.6 %collective-permute-start.6 = (f32[32,128]{1,0:T(8,128)S(1)}, f32[32,128]{1,0:T(8,128)S(1)}, u32[]{:S(2)}, u32[]{:S(2)}) collective-permute-start(f32[32,128]{1,0:T(8,128)S(1)} %get-tuple-element.67), channel_id=1, source_target_pairs={{0,128},{4,132},{8,136},{12,140},{16,144},{20,148},{24,152},{28,15... | collective-permute-start | bytes 49160 | tf_op jit(solution)/shard_map/ppermute | solution.py:383
  63.4 4.2 %collective-permute-start.7 = (f32[32,128]{1,0:T(8,128)S(1)}, f32[32,128]{1,0:T(8,128)S(1)}, u32[]{:S(2)}, u32[]{:S(2)}) collective-permute-start(f32[32,128]{1,0:T(8,128)S(1)} %get-tuple-element.68), channel_id=1, source_target_pairs={{0,384},{4,388},{8,392},{12,396},{16,400},{20,404},{24,408},{28,41... | collective-permute-start | bytes 49160 | tf_op jit(solution)/shard_map/ppermute | solution.py:383
  67.6 1.4 shard_map.116.placed
  69.0 3.9 %collective-permute-done.7.r3 = f32[32,128]{1,0:T(8,128)S(1)} collective-permute-done((f32[32,128]{1,0:T(8,128)S(1)}, f32[32,128]{1,0:T(8,128)S(1)}, u32[]{:S(2)}, u32[]{:S(2)}) %collective-permute-start.7) | collective-permute-done | bytes 16416 | tf_op jit(solution)/shard_map/ppermute | solution.py:383
  73.5 15.6 %all_to_all.45.arrived = f32[4,504,128]{2,1,0:T(8,128)S(1)} all-to-all(f32[4,504,128]{2,1,0:T(8,128)S(1)} %shard_map.117), channel_id=1, replica_groups=mesh['zq'=4,'zr'=4,'x'=4,'core'=2,'sub'=4] {'sub'}, dimensions={0} | all-to-all | bytes 2064384 | tf_op jit(solution)/shard_map/all_to_all | solution.py:481
  89.6 1.9 collective-permute-start.8
  91.5 6.3 %collective-permute-start.9 = (f32[32,128]{1,0:T(8,128)S(1)}, f32[32,128]{1,0:T(8,128)S(1)}, u32[]{:S(2)}, u32[]{:S(2)}) collective-permute-start(f32[32,128]{1,0:T(8,128)S(1)} %get-tuple-element.72), channel_id=1, source_target_pairs={{0,508},{4,8},{8,4},{12,16},{16,12},{20,24},{24,20},{28,32},{32,28... | collective-permute-start | bytes 49160 | tf_op jit(solution)/shard_map/ppermute | solution.py:383
  97.9 2.4 collective-permute-start.10
  100.2 6.2 %collective-permute-start.11 = (f32[32,128]{1,0:T(8,128)S(1)}, f32[32,128]{1,0:T(8,128)S(1)}, u32[]{:S(2)}, u32[]{:S(2)}) collective-permute-start(f32[32,128]{1,0:T(8,128)S(1)} %get-tuple-element.74), channel_id=1, source_target_pairs={{0,384},{4,388},{8,392},{12,396},{16,400},{20,404},{24,408},{28,41... | collective-permute-start | bytes 49160 | tf_op jit(solution)/shard_map/ppermute | solution.py:383
  107.4 2.4 collective-permute-done.11.refs_4_.refs_12_
  109.8 3.4 shard_map.119
  113.2 1.9 collective-permute-start.12
  115.1 4.2 %collective-permute-start.13 = (f32[32,128]{1,0:T(8,128)S(1)}, f32[32,128]{1,0:T(8,128)S(1)}, u32[]{:S(2)}, u32[]{:S(2)}) collective-permute-start(f32[32,128]{1,0:T(8,128)S(1)} %get-tuple-element.77), channel_id=1, source_target_pairs={{0,508},{4,8},{8,4},{12,16},{16,12},{20,24},{24,20},{28,32},{32,28... | collective-permute-start | bytes 49160 | tf_op jit(solution)/shard_map/ppermute | solution.py:383
  119.4 5.1 %collective-permute-start.14 = (f32[32,128]{1,0:T(8,128)S(1)}, f32[32,128]{1,0:T(8,128)S(1)}, u32[]{:S(2)}, u32[]{:S(2)}) collective-permute-start(f32[32,128]{1,0:T(8,128)S(1)} %get-tuple-element.78), channel_id=1, source_target_pairs={{0,128},{4,132},{8,136},{12,140},{16,144},{20,148},{24,152},{28,15... | collective-permute-start | bytes 49160 | tf_op jit(solution)/shard_map/ppermute | solution.py:383
  124.4 3.2 collective-permute-start.15
  127.6 1.4 shard_map.120.placed
  129.0 5.0 %collective-permute-done.15.r3 = f32[32,128]{1,0:T(8,128)S(1)} collective-permute-done((f32[32,128]{1,0:T(8,128)S(1)}, f32[32,128]{1,0:T(8,128)S(1)}, u32[]{:S(2)}, u32[]{:S(2)}) %collective-permute-start.15) | collective-permute-done | bytes 16416 | tf_op jit(solution)/shard_map/ppermute | solution.py:383
  134.6 16.8 %all_to_all.46.arrived = f32[4,504,128]{2,1,0:T(8,128)S(1)} all-to-all(f32[4,504,128]{2,1,0:T(8,128)S(1)} %shard_map.121), channel_id=1, replica_groups=mesh['zq'=4,'zr'=4,'x'=4,'core'=2,'sub'=4] {'sub'}, dimensions={0} | all-to-all | bytes 2064384 | tf_op jit(solution)/shard_map/all_to_all | solution.py:481
  151.9 1.9 collective-permute-start.16
  153.8 4.7 %collective-permute-start.17 = (f32[32,128]{1,0:T(8,128)S(1)}, f32[32,128]{1,0:T(8,128)S(1)}, u32[]{:S(2)}, u32[]{:S(2)}) collective-permute-start(f32[32,128]{1,0:T(8,128)S(1)} %get-tuple-element.82), channel_id=1, source_target_pairs={{0,508},{4,8},{8,4},{12,16},{16,12},{20,24},{24,20},{28,32},{32,28... | collective-permute-start | bytes 49160 | tf_op jit(solution)/shard_map/ppermute | solution.py:383
  158.5 2.1 collective-permute-start.18
  160.7 6.5 %collective-permute-start.19 = (f32[32,128]{1,0:T(8,128)S(1)}, f32[32,128]{1,0:T(8,128)S(1)}, u32[]{:S(2)}, u32[]{:S(2)}) collective-permute-start(f32[32,128]{1,0:T(8,128)S(1)} %get-tuple-element.84), channel_id=1, source_target_pairs={{0,384},{4,388},{8,392},{12,396},{16,400},{20,404},{24,408},{28,41... | collective-permute-start | bytes 49160 | tf_op jit(solution)/shard_map/ppermute | solution.py:383
  168.1 2.1 collective-permute-done.19.refs_4_.refs_16_
  170.2 2.7 shard_map.124
  172.9 11.0 %all_to_all.47.arrived = f32[32,8,128]{2,1,0:T(8,128)S(1)} all-to-all(f32[32,8,128]{2,1,0:T(8,128)S(1)} %shard_map.124), channel_id=1, replica_groups=mesh['zq'=4,'zr'=4,'x'=4,'core'=2,'sub'=4] {'x','core','sub'}, dimensions={0} | all-to-all | bytes 262144 | tf_op jit(solution)/shard_map/all_to_all | solution.py:522
  183.9 20.9 %all_to_all.48.refs_0_ = f32[16,8,128]{2,1,0:T(8,128)S(1)} all-to-all(f32[16,8,128]{2,1,0:T(8,128)S(1)} %shard_map.125), channel_id=1, replica_groups=mesh['zq'=4,'zr'=4,'x'=4,'core'=2,'sub'=4] {'zq','zr'}, dimensions={0} | all-to-all | bytes 131072 | tf_op jit(solution)/shard_map/all_to_all | solution.py:524
  205.2 3.6 shard_map.127
  208.8 1.9 collective-permute-start.20
  210.7 4.1 %collective-permute-start.21 = (f32[32,128]{1,0:T(8,128)S(1)}, f32[32,128]{1,0:T(8,128)S(1)}, u32[]{:S(2)}, u32[]{:S(2)}) collective-permute-start(f32[32,128]{1,0:T(8,128)S(1)} %get-tuple-element.92), channel_id=1, source_target_pairs={{0,508},{4,8},{8,4},{12,16},{16,12},{20,24},{24,20},{28,32},{32,28... | collective-permute-start | bytes 49160 | tf_op jit(solution)/shard_map/ppermute | solution.py:383
  214.9 4.3 %collective-permute-start.22 = (f32[32,128]{1,0:T(8,128)S(1)}, f32[32,128]{1,0:T(8,128)S(1)}, u32[]{:S(2)}, u32[]{:S(2)}) collective-permute-start(f32[32,128]{1,0:T(8,128)S(1)} %get-tuple-element.93), channel_id=1, source_target_pairs={{0,128},{4,132},{8,136},{12,140},{16,144},{20,148},{24,152},{28,15... | collective-permute-start | bytes 49160 | tf_op jit(solution)/shard_map/ppermute | solution.py:383
  219.2 2.9 collective-permute-start.23
  224.7 4.0 %collective-permute-done.23.r3 = f32[32,128]{1,0:T(8,128)S(1)} collective-permute-done((f32[32,128]{1,0:T(8,128)S(1)}, f32[32,128]{1,0:T(8,128)S(1)}, u32[]{:S(2)}, u32[]{:S(2)}) %collective-permute-start.23) | collective-permute-done | bytes 16416 | tf_op jit(solution)/shard_map/ppermute | solution.py:383
  229.3 13.9 %all_to_all.49.arrived = f32[4,504,128]{2,1,0:T(8,128)S(1)} all-to-all(f32[4,504,128]{2,1,0:T(8,128)S(1)} %shard_map.129), channel_id=1, replica_groups=mesh['zq'=4,'zr'=4,'x'=4,'core'=2,'sub'=4] {'sub'}, dimensions={0} | all-to-all | bytes 2064384 | tf_op jit(solution)/shard_map/all_to_all | solution.py:481
  243.7 1.9 collective-permute-start.24
  245.6 5.0 %collective-permute-start.25 = (f32[32,128]{1,0:T(8,128)S(1)}, f32[32,128]{1,0:T(8,128)S(1)}, u32[]{:S(2)}, u32[]{:S(2)}) collective-permute-start(f32[32,128]{1,0:T(8,128)S(1)} %get-tuple-element.97), channel_id=1, source_target_pairs={{0,508},{4,8},{8,4},{12,16},{16,12},{20,24},{24,20},{28,32},{32,28... | collective-permute-start | bytes 49160 | tf_op jit(solution)/shard_map/ppermute | solution.py:383
  250.6 4.6 %collective-permute-start.26 = (f32[32,128]{1,0:T(8,128)S(1)}, f32[32,128]{1,0:T(8,128)S(1)}, u32[]{:S(2)}, u32[]{:S(2)}) collective-permute-start(f32[32,128]{1,0:T(8,128)S(1)} %get-tuple-element.98), channel_id=1, source_target_pairs={{0,128},{4,132},{8,136},{12,140},{16,144},{20,148},{24,152},{28,15... | collective-permute-start | bytes 49160 | tf_op jit(solution)/shard_map/ppermute | solution.py:383
  255.2 7.0 %collective-permute-start.27 = (f32[32,128]{1,0:T(8,128)S(1)}, f32[32,128]{1,0:T(8,128)S(1)}, u32[]{:S(2)}, u32[]{:S(2)}) collective-permute-start(f32[32,128]{1,0:T(8,128)S(1)} %get-tuple-element.99), channel_id=1, source_target_pairs={{0,384},{4,388},{8,392},{12,396},{16,400},{20,404},{24,408},{28,41... | collective-permute-start | bytes 49160 | tf_op jit(solution)/shard_map/ppermute | solution.py:383
  262.3 2.5 collective-permute-done.27.refs_4_
  264.8 3.5 shard_map.131
  268.3 1.9 collective-permute-start.28
  270.2 5.7 %collective-permute-start.29 = (f32[32,128]{1,0:T(8,128)S(1)}, f32[32,128]{1,0:T(8,128)S(1)}, u32[]{:S(2)}, u32[]{:S(2)}) collective-permute-start(f32[32,128]{1,0:T(8,128)S(1)} %get-tuple-element.102), channel_id=1, source_target_pairs={{0,508},{4,8},{8,4},{12,16},{16,12},{20,24},{24,20},{28,32},{32,28... | collective-permute-start | bytes 49160 | tf_op jit(solution)/shard_map/ppermute | solution.py:383
  275.9 3.2 collective-permute-start.30
  279.2 6.5 %collective-permute-start.31 = (f32[32,128]{1,0:T(8,128)S(1)}, f32[32,128]{1,0:T(8,128)S(1)}, u32[]{:S(2)}, u32[]{:S(2)}) collective-permute-start(f32[32,128]{1,0:T(8,128)S(1)} %get-tuple-element.104), channel_id=1, source_target_pairs={{0,384},{4,388},{8,392},{12,396},{16,400},{20,404},{24,408},{28,41... | collective-permute-start | bytes 49160 | tf_op jit(solution)/shard_map/ppermute | solution.py:383
  285.6 1.4 shard_map.132.placed
  287.1 1.6 collective-permute-done.31.r3
  289.3 16.1 %all_to_all.50.arrived = f32[4,504,128]{2,1,0:T(8,128)S(1)} all-to-all(f32[4,504,128]{2,1,0:T(8,128)S(1)} %shard_map.133), channel_id=1, replica_groups=mesh['zq'=4,'zr'=4,'x'=4,'core'=2,'sub'=4] {'sub'}, dimensions={0} | all-to-all | bytes 2064384 | tf_op jit(solution)/shard_map/all_to_all | solution.py:481
  305.9 1.9 collective-permute-start.32
  307.8 3.6 collective-permute-start.33
  311.4 6.0 %collective-permute-start.34 = (f32[32,128]{1,0:T(8,128)S(1)}, f32[32,128]{1,0:T(8,128)S(1)}, u32[]{:S(2)}, u32[]{:S(2)}) collective-permute-start(f32[32,128]{1,0:T(8,128)S(1)} %get-tuple-element.108), channel_id=1, source_target_pairs={{0,128},{4,132},{8,136},{12,140},{16,144},{20,148},{24,152},{28,15... | collective-permute-start | bytes 49160 | tf_op jit(solution)/shard_map/ppermute | solution.py:383
  317.4 4.8 %collective-permute-start.35 = (f32[32,128]{1,0:T(8,128)S(1)}, f32[32,128]{1,0:T(8,128)S(1)}, u32[]{:S(2)}, u32[]{:S(2)}) collective-permute-start(f32[32,128]{1,0:T(8,128)S(1)} %get-tuple-element.109), channel_id=1, source_target_pairs={{0,384},{4,388},{8,392},{12,396},{16,400},{20,404},{24,408},{28,41... | collective-permute-start | bytes 49160 | tf_op jit(solution)/shard_map/ppermute | solution.py:383
  322.5 4.5 %collective-permute-done.35.refs_4_ = f32[32,128]{1,0:T(8,128)S(1)} collective-permute-done((f32[32,128]{1,0:T(8,128)S(1)}, f32[32,128]{1,0:T(8,128)S(1)}, u32[]{:S(2)}, u32[]{:S(2)}) %collective-permute-start.35) | collective-permute-done | bytes 16416 | tf_op jit(solution)/shard_map/ppermute | solution.py:383
  327.0 2.7 shard_map.136
  330.5 11.1 %all_to_all.51.arrived = f32[32,8,128]{2,1,0:T(8,128)S(1)} all-to-all(f32[32,8,128]{2,1,0:T(8,128)S(1)} %get-tuple-element.110), channel_id=1, replica_groups=mesh['zq'=4,'zr'=4,'x'=4,'core'=2,'sub'=4] {'x','core','sub'}, dimensions={0} | all-to-all | bytes 262144 | tf_op jit(solution)/shard_map/all_to_all | solution.py:522
  342.2 7.7 %all-to-all-start.8 = ((f32[16,8,128]{2,1,0:T(8,128)}), f32[16,8,128]{2,1,0:T(8,128)S(1)}, u32[]{:S(2)}, u32[]{:S(2)}) async-start(f32[16,8,128]{2,1,0:T(8,128)} %shard_map.137), calls=%async_computation.8 | async-start | bytes 131072 | tf_op jit(solution)/shard_map/all_to_all | solution.py:524
  349.9 12.7 %all-to-all-done.8.arrived = f32[16,8,128]{2,1,0:T(8,128)S(1)} async-done(((f32[16,8,128]{2,1,0:T(8,128)}), f32[16,8,128]{2,1,0:T(8,128)S(1)}, u32[]{:S(2)}, u32[]{:S(2)}) %all-to-all-start.8) | async-done | bytes 65568 | tf_op jit(solution)/shard_map/all_to_all | solution.py:524
  (99 shorter events, 25.8 us)
Async XLA Ops:
  0.6 0.9 copy-start.6
  1.5 0.9 copy-start.7
  2.4 0.7 copy-start.9
  4.3 9.9 %copy-start.12 = (f32[500,150]{0,1:T(8,128)S(1)}, f32[500,150]{0,1:T(8,128)}, u32[]{:S(2)}) copy-start(f32[500,150]{0,1:T(8,128)} %param.15) | copy-start | bytes 900004
  4.3 10.0 %copy-start.10 = (f32[500,500]{1,0:T(8,128)S(1)}, f32[500,500]{1,0:T(8,128)}, u32[]{:S(2)}) copy-start(f32[500,500]{1,0:T(8,128)} %param.16) | copy-start | bytes 3000004
  4.3 16.5 %all-to-all-start = ((f32[4,64,640]{2,1,0:T(8,128)}), f32[4,64,640]{2,1,0:T(8,128)S(1)}, u32[]{:S(2)}, u32[]{:S(2)}) async-start(f32[4,64,640]{2,1,0:T(8,128)} %shard_map.113), calls=%async_computation | async-start | bytes 1310720 | tf_op jit(solution)/shard_map/all_to_all | solution.py:438
  13.4 0.7 copy-start.14
  15.2 0.7 copy-start.16
  15.9 0.7 copy-start.15
  16.8 1.0 copy-start.13
  19.6 1.0 copy-start.11
  21.9 21.6 %collective-permute-start = (f32[64,128]{1,0:T(8,128)S(1)}, f32[64,128]{1,0:T(8,128)S(1)}, u32[]{:S(2)}, u32[]{:S(2)}) collective-permute-start(f32[64,128]{1,0:T(8,128)S(1)} %get-tuple-element.60), channel_id=1, source_target_pairs={{0,4},{4,0},{8,12},{12,8},{16,20},{20,16},{24,28},{28,24},{32,36},... | collective-permute-start | bytes 98312 | tf_op jit(solution)/shard_map/ppermute | solution.py:383
  23.8 19.7 %collective-permute-start.1 = (f32[64,128]{1,0:T(8,128)S(1)}, f32[64,128]{1,0:T(8,128)S(1)}, u32[]{:S(2)}, u32[]{:S(2)}) collective-permute-start(f32[64,128]{1,0:T(8,128)S(1)} %get-tuple-element.61), channel_id=1, source_target_pairs={{0,508},{4,8},{8,4},{12,16},{16,12},{20,24},{24,20},{28,32},{32,28... | collective-permute-start | bytes 98312 | tf_op jit(solution)/shard_map/ppermute | solution.py:383
  34.7 9.8 %collective-permute-start.2 = (f32[64,128]{1,0:T(8,128)S(1)}, f32[64,128]{1,0:T(8,128)S(1)}, u32[]{:S(2)}, u32[]{:S(2)}) collective-permute-start(f32[64,128]{1,0:T(8,128)S(1)} %get-tuple-element.62), channel_id=1, source_target_pairs={{0,128},{4,132},{8,136},{12,140},{16,144},{20,148},{24,152},{28,15... | collective-permute-start | bytes 98312 | tf_op jit(solution)/shard_map/ppermute | solution.py:383
  36.7 9.7 %collective-permute-start.3 = (f32[64,128]{1,0:T(8,128)S(1)}, f32[64,128]{1,0:T(8,128)S(1)}, u32[]{:S(2)}, u32[]{:S(2)}) collective-permute-start(f32[64,128]{1,0:T(8,128)S(1)} %get-tuple-element.63), channel_id=1, source_target_pairs={{0,384},{4,388},{8,392},{12,396},{16,400},{20,404},{24,408},{28,41... | collective-permute-start | bytes 98312 | tf_op jit(solution)/shard_map/ppermute | solution.py:383
  46.4 0.7 copy-start.8
  50.5 18.6 %collective-permute-start.4 = (f32[32,128]{1,0:T(8,128)S(1)}, f32[32,128]{1,0:T(8,128)S(1)}, u32[]{:S(2)}, u32[]{:S(2)}) collective-permute-start(f32[32,128]{1,0:T(8,128)S(1)} %get-tuple-element.65), channel_id=1, source_target_pairs={{0,4},{4,0},{8,12},{12,8},{16,20},{20,16},{24,28},{28,24},{32,36},... | collective-permute-start | bytes 49160 | tf_op jit(solution)/shard_map/ppermute | solution.py:383
  52.4 16.6 %collective-permute-start.5 = (f32[32,128]{1,0:T(8,128)S(1)}, f32[32,128]{1,0:T(8,128)S(1)}, u32[]{:S(2)}, u32[]{:S(2)}) collective-permute-start(f32[32,128]{1,0:T(8,128)S(1)} %get-tuple-element.66), channel_id=1, source_target_pairs={{0,508},{4,8},{8,4},{12,16},{16,12},{20,24},{24,20},{28,32},{32,28... | collective-permute-start | bytes 49160 | tf_op jit(solution)/shard_map/ppermute | solution.py:383
  58.8 10.3 %collective-permute-start.6 = (f32[32,128]{1,0:T(8,128)S(1)}, f32[32,128]{1,0:T(8,128)S(1)}, u32[]{:S(2)}, u32[]{:S(2)}) collective-permute-start(f32[32,128]{1,0:T(8,128)S(1)} %get-tuple-element.67), channel_id=1, source_target_pairs={{0,128},{4,132},{8,136},{12,140},{16,144},{20,148},{24,152},{28,15... | collective-permute-start | bytes 49160 | tf_op jit(solution)/shard_map/ppermute | solution.py:383
  63.4 9.5 %collective-permute-start.7 = (f32[32,128]{1,0:T(8,128)S(1)}, f32[32,128]{1,0:T(8,128)S(1)}, u32[]{:S(2)}, u32[]{:S(2)}) collective-permute-start(f32[32,128]{1,0:T(8,128)S(1)} %get-tuple-element.68), channel_id=1, source_target_pairs={{0,384},{4,388},{8,392},{12,396},{16,400},{20,404},{24,408},{28,41... | collective-permute-start | bytes 49160 | tf_op jit(solution)/shard_map/ppermute | solution.py:383
  89.6 16.9 %collective-permute-start.8 = (f32[32,128]{1,0:T(8,128)S(1)}, f32[32,128]{1,0:T(8,128)S(1)}, u32[]{:S(2)}, u32[]{:S(2)}) collective-permute-start(f32[32,128]{1,0:T(8,128)S(1)} %get-tuple-element.71), channel_id=1, source_target_pairs={{0,4},{4,0},{8,12},{12,8},{16,20},{20,16},{24,28},{28,24},{32,36},... | collective-permute-start | bytes 49160 | tf_op jit(solution)/shard_map/ppermute | solution.py:383
  91.5 15.0 %collective-permute-start.9 = (f32[32,128]{1,0:T(8,128)S(1)}, f32[32,128]{1,0:T(8,128)S(1)}, u32[]{:S(2)}, u32[]{:S(2)}) collective-permute-start(f32[32,128]{1,0:T(8,128)S(1)} %get-tuple-element.72), channel_id=1, source_target_pairs={{0,508},{4,8},{8,4},{12,16},{16,12},{20,24},{24,20},{28,32},{32,28... | collective-permute-start | bytes 49160 | tf_op jit(solution)/shard_map/ppermute | solution.py:383
  97.9 9.5 %collective-permute-start.10 = (f32[32,128]{1,0:T(8,128)S(1)}, f32[32,128]{1,0:T(8,128)S(1)}, u32[]{:S(2)}, u32[]{:S(2)}) collective-permute-start(f32[32,128]{1,0:T(8,128)S(1)} %get-tuple-element.73), channel_id=1, source_target_pairs={{0,128},{4,132},{8,136},{12,140},{16,144},{20,148},{24,152},{28,15... | collective-permute-start | bytes 49160 | tf_op jit(solution)/shard_map/ppermute | solution.py:383
  100.2 9.5 %collective-permute-start.11 = (f32[32,128]{1,0:T(8,128)S(1)}, f32[32,128]{1,0:T(8,128)S(1)}, u32[]{:S(2)}, u32[]{:S(2)}) collective-permute-start(f32[32,128]{1,0:T(8,128)S(1)} %get-tuple-element.74), channel_id=1, source_target_pairs={{0,384},{4,388},{8,392},{12,396},{16,400},{20,404},{24,408},{28,41... | collective-permute-start | bytes 49160 | tf_op jit(solution)/shard_map/ppermute | solution.py:383
  113.2 15.8 %collective-permute-start.12 = (f32[32,128]{1,0:T(8,128)S(1)}, f32[32,128]{1,0:T(8,128)S(1)}, u32[]{:S(2)}, u32[]{:S(2)}) collective-permute-start(f32[32,128]{1,0:T(8,128)S(1)} %get-tuple-element.76), channel_id=1, source_target_pairs={{0,4},{4,0},{8,12},{12,8},{16,20},{20,16},{24,28},{28,24},{32,36},... | collective-permute-start | bytes 49160 | tf_op jit(solution)/shard_map/ppermute | solution.py:383
  115.1 13.9 %collective-permute-start.13 = (f32[32,128]{1,0:T(8,128)S(1)}, f32[32,128]{1,0:T(8,128)S(1)}, u32[]{:S(2)}, u32[]{:S(2)}) collective-permute-start(f32[32,128]{1,0:T(8,128)S(1)} %get-tuple-element.77), channel_id=1, source_target_pairs={{0,508},{4,8},{8,4},{12,16},{16,12},{20,24},{24,20},{28,32},{32,28... | collective-permute-start | bytes 49160 | tf_op jit(solution)/shard_map/ppermute | solution.py:383
  119.4 9.7 %collective-permute-start.14 = (f32[32,128]{1,0:T(8,128)S(1)}, f32[32,128]{1,0:T(8,128)S(1)}, u32[]{:S(2)}, u32[]{:S(2)}) collective-permute-start(f32[32,128]{1,0:T(8,128)S(1)} %get-tuple-element.78), channel_id=1, source_target_pairs={{0,128},{4,132},{8,136},{12,140},{16,144},{20,148},{24,152},{28,15... | collective-permute-start | bytes 49160 | tf_op jit(solution)/shard_map/ppermute | solution.py:383
  124.4 9.5 %collective-permute-start.15 = (f32[32,128]{1,0:T(8,128)S(1)}, f32[32,128]{1,0:T(8,128)S(1)}, u32[]{:S(2)}, u32[]{:S(2)}) collective-permute-start(f32[32,128]{1,0:T(8,128)S(1)} %get-tuple-element.79), channel_id=1, source_target_pairs={{0,384},{4,388},{8,392},{12,396},{16,400},{20,404},{24,408},{28,41... | collective-permute-start | bytes 49160 | tf_op jit(solution)/shard_map/ppermute | solution.py:383
  151.9 15.5 %collective-permute-start.16 = (f32[32,128]{1,0:T(8,128)S(1)}, f32[32,128]{1,0:T(8,128)S(1)}, u32[]{:S(2)}, u32[]{:S(2)}) collective-permute-start(f32[32,128]{1,0:T(8,128)S(1)} %get-tuple-element.81), channel_id=1, source_target_pairs={{0,4},{4,0},{8,12},{12,8},{16,20},{20,16},{24,28},{28,24},{32,36},... | collective-permute-start | bytes 49160 | tf_op jit(solution)/shard_map/ppermute | solution.py:383
  153.8 13.6 %collective-permute-start.17 = (f32[32,128]{1,0:T(8,128)S(1)}, f32[32,128]{1,0:T(8,128)S(1)}, u32[]{:S(2)}, u32[]{:S(2)}) collective-permute-start(f32[32,128]{1,0:T(8,128)S(1)} %get-tuple-element.82), channel_id=1, source_target_pairs={{0,508},{4,8},{8,4},{12,16},{16,12},{20,24},{24,20},{28,32},{32,28... | collective-permute-start | bytes 49160 | tf_op jit(solution)/shard_map/ppermute | solution.py:383
  158.5 9.5 %collective-permute-start.18 = (f32[32,128]{1,0:T(8,128)S(1)}, f32[32,128]{1,0:T(8,128)S(1)}, u32[]{:S(2)}, u32[]{:S(2)}) collective-permute-start(f32[32,128]{1,0:T(8,128)S(1)} %get-tuple-element.83), channel_id=1, source_target_pairs={{0,128},{4,132},{8,136},{12,140},{16,144},{20,148},{24,152},{28,15... | collective-permute-start | bytes 49160 | tf_op jit(solution)/shard_map/ppermute | solution.py:383
  160.7 9.5 %collective-permute-start.19 = (f32[32,128]{1,0:T(8,128)S(1)}, f32[32,128]{1,0:T(8,128)S(1)}, u32[]{:S(2)}, u32[]{:S(2)}) collective-permute-start(f32[32,128]{1,0:T(8,128)S(1)} %get-tuple-element.84), channel_id=1, source_target_pairs={{0,384},{4,388},{8,392},{12,396},{16,400},{20,404},{24,408},{28,41... | collective-permute-start | bytes 49160 | tf_op jit(solution)/shard_map/ppermute | solution.py:383
  208.8 14.6 %copy-start = (f32[512,256]{1,0:T(8,128)}, f32[512,256]{1,0:T(8,128)S(1)}, u32[]{:S(2)}) copy-start(f32[512,256]{1,0:T(8,128)S(1)} %get-tuple-element.113) | copy-start | bytes 1572868
  208.8 14.6 %collective-permute-start.20 = (f32[32,128]{1,0:T(8,128)S(1)}, f32[32,128]{1,0:T(8,128)S(1)}, u32[]{:S(2)}, u32[]{:S(2)}) collective-permute-start(f32[32,128]{1,0:T(8,128)S(1)} %get-tuple-element.91), channel_id=1, source_target_pairs={{0,4},{4,0},{8,12},{12,8},{16,20},{20,16},{24,28},{28,24},{32,36},... | collective-permute-start | bytes 49160 | tf_op jit(solution)/shard_map/ppermute | solution.py:383
  210.7 12.7 %collective-permute-start.21 = (f32[32,128]{1,0:T(8,128)S(1)}, f32[32,128]{1,0:T(8,128)S(1)}, u32[]{:S(2)}, u32[]{:S(2)}) collective-permute-start(f32[32,128]{1,0:T(8,128)S(1)} %get-tuple-element.92), channel_id=1, source_target_pairs={{0,508},{4,8},{8,4},{12,16},{16,12},{20,24},{24,20},{28,32},{32,28... | collective-permute-start | bytes 49160 | tf_op jit(solution)/shard_map/ppermute | solution.py:383
  214.9 9.8 %collective-permute-start.22 = (f32[32,128]{1,0:T(8,128)S(1)}, f32[32,128]{1,0:T(8,128)S(1)}, u32[]{:S(2)}, u32[]{:S(2)}) collective-permute-start(f32[32,128]{1,0:T(8,128)S(1)} %get-tuple-element.93), channel_id=1, source_target_pairs={{0,128},{4,132},{8,136},{12,140},{16,144},{20,148},{24,152},{28,15... | collective-permute-start | bytes 49160 | tf_op jit(solution)/shard_map/ppermute | solution.py:383
  219.2 9.5 %collective-permute-start.23 = (f32[32,128]{1,0:T(8,128)S(1)}, f32[32,128]{1,0:T(8,128)S(1)}, u32[]{:S(2)}, u32[]{:S(2)}) collective-permute-start(f32[32,128]{1,0:T(8,128)S(1)} %get-tuple-element.94), channel_id=1, source_target_pairs={{0,384},{4,388},{8,392},{12,396},{16,400},{20,404},{24,408},{28,41... | collective-permute-start | bytes 49160 | tf_op jit(solution)/shard_map/ppermute | solution.py:383
  243.7 18.6 %collective-permute-start.24 = (f32[32,128]{1,0:T(8,128)S(1)}, f32[32,128]{1,0:T(8,128)S(1)}, u32[]{:S(2)}, u32[]{:S(2)}) collective-permute-start(f32[32,128]{1,0:T(8,128)S(1)} %get-tuple-element.96), channel_id=1, source_target_pairs={{0,4},{4,0},{8,12},{12,8},{16,20},{20,16},{24,28},{28,24},{32,36},... | collective-permute-start | bytes 49160 | tf_op jit(solution)/shard_map/ppermute | solution.py:383
  245.6 16.6 %collective-permute-start.25 = (f32[32,128]{1,0:T(8,128)S(1)}, f32[32,128]{1,0:T(8,128)S(1)}, u32[]{:S(2)}, u32[]{:S(2)}) collective-permute-start(f32[32,128]{1,0:T(8,128)S(1)} %get-tuple-element.97), channel_id=1, source_target_pairs={{0,508},{4,8},{8,4},{12,16},{16,12},{20,24},{24,20},{28,32},{32,28... | collective-permute-start | bytes 49160 | tf_op jit(solution)/shard_map/ppermute | solution.py:383
  250.6 11.6 %collective-permute-start.26 = (f32[32,128]{1,0:T(8,128)S(1)}, f32[32,128]{1,0:T(8,128)S(1)}, u32[]{:S(2)}, u32[]{:S(2)}) collective-permute-start(f32[32,128]{1,0:T(8,128)S(1)} %get-tuple-element.98), channel_id=1, source_target_pairs={{0,128},{4,132},{8,136},{12,140},{16,144},{20,148},{24,152},{28,15... | collective-permute-start | bytes 49160 | tf_op jit(solution)/shard_map/ppermute | solution.py:383
  255.2 9.5 %collective-permute-start.27 = (f32[32,128]{1,0:T(8,128)S(1)}, f32[32,128]{1,0:T(8,128)S(1)}, u32[]{:S(2)}, u32[]{:S(2)}) collective-permute-start(f32[32,128]{1,0:T(8,128)S(1)} %get-tuple-element.99), channel_id=1, source_target_pairs={{0,384},{4,388},{8,392},{12,396},{16,400},{20,404},{24,408},{28,41... | collective-permute-start | bytes 49160 | tf_op jit(solution)/shard_map/ppermute | solution.py:383
  268.3 18.7 %copy-start.2 = (f32[512,256]{1,0:T(8,128)}, f32[512,256]{1,0:T(8,128)S(1)}, u32[]{:S(2)}) copy-start(f32[512,256]{1,0:T(8,128)S(1)} %get-tuple-element.114) | copy-start | bytes 1572868
  268.3 18.7 %collective-permute-start.28 = (f32[32,128]{1,0:T(8,128)S(1)}, f32[32,128]{1,0:T(8,128)S(1)}, u32[]{:S(2)}, u32[]{:S(2)}) collective-permute-start(f32[32,128]{1,0:T(8,128)S(1)} %get-tuple-element.101), channel_id=1, source_target_pairs={{0,4},{4,0},{8,12},{12,8},{16,20},{20,16},{24,28},{28,24},{32,36},... | collective-permute-start | bytes 49160 | tf_op jit(solution)/shard_map/ppermute | solution.py:383
  270.2 16.8 %collective-permute-start.29 = (f32[32,128]{1,0:T(8,128)S(1)}, f32[32,128]{1,0:T(8,128)S(1)}, u32[]{:S(2)}, u32[]{:S(2)}) collective-permute-start(f32[32,128]{1,0:T(8,128)S(1)} %get-tuple-element.102), channel_id=1, source_target_pairs={{0,508},{4,8},{8,4},{12,16},{16,12},{20,24},{24,20},{28,32},{32,28... | collective-permute-start | bytes 49160 | tf_op jit(solution)/shard_map/ppermute | solution.py:383
  275.9 11.1 %collective-permute-start.30 = (f32[32,128]{1,0:T(8,128)S(1)}, f32[32,128]{1,0:T(8,128)S(1)}, u32[]{:S(2)}, u32[]{:S(2)}) collective-permute-start(f32[32,128]{1,0:T(8,128)S(1)} %get-tuple-element.103), channel_id=1, source_target_pairs={{0,128},{4,132},{8,136},{12,140},{16,144},{20,148},{24,152},{28,15... | collective-permute-start | bytes 49160 | tf_op jit(solution)/shard_map/ppermute | solution.py:383
  279.2 9.5 %collective-permute-start.31 = (f32[32,128]{1,0:T(8,128)S(1)}, f32[32,128]{1,0:T(8,128)S(1)}, u32[]{:S(2)}, u32[]{:S(2)}) collective-permute-start(f32[32,128]{1,0:T(8,128)S(1)} %get-tuple-element.104), channel_id=1, source_target_pairs={{0,384},{4,388},{8,392},{12,396},{16,400},{20,404},{24,408},{28,41... | collective-permute-start | bytes 49160 | tf_op jit(solution)/shard_map/ppermute | solution.py:383
  305.9 16.6 %collective-permute-start.32 = (f32[32,128]{1,0:T(8,128)S(1)}, f32[32,128]{1,0:T(8,128)S(1)}, u32[]{:S(2)}, u32[]{:S(2)}) collective-permute-start(f32[32,128]{1,0:T(8,128)S(1)} %get-tuple-element.106), channel_id=1, source_target_pairs={{0,4},{4,0},{8,12},{12,8},{16,20},{20,16},{24,28},{28,24},{32,36},... | collective-permute-start | bytes 49160 | tf_op jit(solution)/shard_map/ppermute | solution.py:383
  307.8 14.7 %collective-permute-start.33 = (f32[32,128]{1,0:T(8,128)S(1)}, f32[32,128]{1,0:T(8,128)S(1)}, u32[]{:S(2)}, u32[]{:S(2)}) collective-permute-start(f32[32,128]{1,0:T(8,128)S(1)} %get-tuple-element.107), channel_id=1, source_target_pairs={{0,508},{4,8},{8,4},{12,16},{16,12},{20,24},{24,20},{28,32},{32,28... | collective-permute-start | bytes 49160 | tf_op jit(solution)/shard_map/ppermute | solution.py:383
  311.4 11.1 %collective-permute-start.34 = (f32[32,128]{1,0:T(8,128)S(1)}, f32[32,128]{1,0:T(8,128)S(1)}, u32[]{:S(2)}, u32[]{:S(2)}) collective-permute-start(f32[32,128]{1,0:T(8,128)S(1)} %get-tuple-element.108), channel_id=1, source_target_pairs={{0,128},{4,132},{8,136},{12,140},{16,144},{20,148},{24,152},{28,15... | collective-permute-start | bytes 49160 | tf_op jit(solution)/shard_map/ppermute | solution.py:383
  317.4 9.5 %collective-permute-start.35 = (f32[32,128]{1,0:T(8,128)S(1)}, f32[32,128]{1,0:T(8,128)S(1)}, u32[]{:S(2)}, u32[]{:S(2)}) collective-permute-start(f32[32,128]{1,0:T(8,128)S(1)} %get-tuple-element.109), channel_id=1, source_target_pairs={{0,384},{4,388},{8,392},{12,396},{16,400},{20,404},{24,408},{28,41... | collective-permute-start | bytes 49160 | tf_op jit(solution)/shard_map/ppermute | solution.py:383
  329.6 0.8 copy-start.4
  330.4 33.1 %copy-start.5 = (f32[512,256]{1,0:T(8,128)S(1)}, f32[512,256]{1,0:T(8,128)}, u32[]{:S(2)}) copy-start(f32[512,256]{1,0:T(8,128)} %copy-done.4) | copy-start | bytes 1572868
  342.2 20.5 %all-to-all-start.8 = ((f32[16,8,128]{2,1,0:T(8,128)}), f32[16,8,128]{2,1,0:T(8,128)S(1)}, u32[]{:S(2)}, u32[]{:S(2)}) async-start(f32[16,8,128]{2,1,0:T(8,128)} %shard_map.137), calls=%async_computation.8 | async-start | bytes 131072 | tf_op jit(solution)/shard_map/all_to_all | solution.py:524
  362.7 1.0 copy-start.1
  362.7 1.2 copy-start.3
